TPU v7x, 256 devices: a whole 4x4x8 slice. The times are simulated.
256 devices in a mesh: dp: 4 (over x), expert: 64 (over y, z, core).
Axes of the slice: x: 4, y: 4, z: 8, core: 2. Of those that a mesh axis runs over, the one named last changes fastest.
Arguments:
- hidden: bfloat16 [4, 4096, 2, 2048], P('dp', 'expert'), may hold values from -6 to 6
- queries: bfloat16 [4, 4096, 2, 4096], P('dp', 'expert'), may hold values from -45 to 45
- latents: bfloat16 [4, 4096, 2, 512], P('dp', 'expert'), may hold values from -165 to 165
- mem_latents: bfloat16 [4, 32, 2, 512], P('dp'), may hold values from -6 to 6
- lengths: int32 [4, 2], P('dp'), may hold values from 2048 to 4096
- ids: int32 [4, 4096, 2, 6], P('dp', 'expert'), may hold values from 0 to 63, all different within a row; in each aligned block of 128 rows (0 to 127, 128 to 255, ..., all dimensions but the last counted through in order) at most 14 rows name the same one
- gates: bfloat16 [4, 4096, 2, 6], P('dp', 'expert'), may hold values from 0.049804688 to 0.5
- norm_gain: bfloat16 [2048], replicated, may hold values from 0.25 to 1.75
- w_uv: bfloat16 [8, 512, 128], P('dp'), may hold values from -0.25 to 0.25
- w_out: bfloat16 [1024, 2048], P('dp'), may hold values from -0.1875 to 0.1875
- w_gate: bfloat16 [64, 2048, 704], P('expert'), may hold values from -0.125 to 0.125
- w_up: bfloat16 [64, 2048, 704], P('expert'), may hold values from -0.125 to 0.125
- w_down: bfloat16 [64, 704, 2048], P('expert'), may hold values from -0.21875 to 0.21875
Outputs:
- layer_out: bfloat16 [4, 4096, 2, 2048], P('dp', 'expert')
Inputs may be any that keep to these rules, and one draw needn't show every extreme that they name: `ids`: each row names 6 different experts; the rows of one device (aligned blocks of 128 rows in the order of the leading dimensions) name any one expert at most 14 times, a bound that some block reaches.
All inputs are finite; a program needn't handle non-finite values.
Results may differ from a plain program's by a relative error of at most 0.007.
Values may be sent and summed in bfloat16 or wider, within the bound.
A program may use at most 128 MiB of HBM per device.

v0:
```python
import jax
import jax.numpy as jnp
from jax import lax
from jax.sharding import PartitionSpec as P

score_scale = 192.0 ** (-0.5)
norm_eps = 1e-06


def sent_to_all(shard, axis):
    devices = lax.axis_size(axis)
    return lax.all_to_all(
        jnp.broadcast_to(shard[None], (devices, *shard.shape)), axis, 0, 0, tiled=True
    )


def joined_along(blocks, dim):
    dims = list(blocks.shape[1:])
    dims[dim] *= blocks.shape[0]
    return jnp.moveaxis(blocks, 0, dim).reshape(dims)


def gather_directly(shard, axis, dim):
    blocks = sent_to_all(shard, axis)
    return joined_along(blocks, dim)


def shards(
    hidden,
    queries,
    latents,
    mem_latents,
    lengths,
    ids,
    gates,
    norm_gain,
    w_uv,
    w_out,
    w_gate,
    w_up,
    w_down,
):
    local_len = hidden.shape[1]
    seq_count = hidden.shape[2]
    model_width = hidden.shape[3]
    latent_dim = latents.shape[3]
    head_count = queries.shape[3] // latent_dim
    row_count = local_len * seq_count
    owner_count = lax.axis_size("expert")
    shard_index = lax.axis_index("expert")
    own_pos = shard_index * local_len + jnp.arange(local_len, dtype=jnp.int32)
    query_rows = queries[0].reshape(local_len, seq_count, head_count, latent_dim)
    memory = mem_latents[0]
    seq_limit = lengths[0]
    mem_scores = (
        jnp.einsum("tshl,msl->shtm", query_rows, memory, preferred_element_type=jnp.float32)
        * score_scale
    )
    first_max = jnp.max(mem_scores, axis=3)
    mem_weights = jnp.exp(mem_scores - first_max[..., None])
    first_sum = jnp.sum(mem_weights, axis=3)
    first_acc = jnp.einsum(
        "shtm,msl->tshl",
        mem_weights.astype(jnp.bfloat16),
        memory,
        preferred_element_type=jnp.float32,
    )

    def fold_step(carry, portion):
        old_max, old_sum, old_acc = carry
        key_rows = portion[0]
        key_pos = jnp.arange(key_rows.shape[0], dtype=jnp.int32)
        scores = (
            jnp.einsum("tshl,jsl->shtj", query_rows, key_rows, preferred_element_type=jnp.float32)
            * score_scale
        )
        causal = key_pos[None, :] <= own_pos[:, None]
        inside = key_pos[None, :] < seq_limit[:, None]
        visible = causal[None, None, :, :] & inside[:, None, None, :]
        scores = jnp.where(visible, scores, -jnp.inf)
        new_max = jnp.maximum(old_max, jnp.max(scores, axis=3))
        weights = jnp.exp(scores - new_max[..., None])
        factor = jnp.exp(old_max - new_max)
        new_sum = old_sum * factor + jnp.sum(weights, axis=3)
        contrib = jnp.einsum(
            "shtj,jsl->tshl",
            weights.astype(jnp.bfloat16),
            key_rows,
            preferred_element_type=jnp.float32,
        )
        new_acc = old_acc * jnp.transpose(factor, (2, 0, 1))[..., None] + contrib
        return (new_max, new_sum, new_acc)

    portion = lax.all_gather(latents, "expert", axis=1, tiled=True)
    last_pos = jnp.max(own_pos)
    final_max, final_sum, final_acc = lax.cond(
        jnp.int32(0) <= last_pos,
        lambda state: fold_step(state, portion),
        lambda state: state,
        (first_max, first_sum, first_acc),
    )
    attended = (final_acc / jnp.transpose(final_sum, (2, 0, 1))[..., None]).astype(jnp.bfloat16)
    values = jnp.einsum(
        "tshl,hlv->tshv",
        attended,
        gather_directly(w_uv, "dp", 0),
        preferred_element_type=jnp.float32,
    ).astype(jnp.bfloat16)
    flat_values = values.reshape(row_count, -1)
    attn_out = jnp.dot(
        flat_values,
        lax.all_gather(w_out, "dp", axis=0, tiled=True),
        preferred_element_type=jnp.float32,
    )
    residual = hidden[0].reshape(row_count, model_width).astype(jnp.float32) + attn_out
    mean_square = jnp.mean(residual * residual, axis=-1, keepdims=True)
    normed = (residual * lax.rsqrt(mean_square + norm_eps) * norm_gain.astype(jnp.float32)).astype(
        jnp.bfloat16
    )
    experts_here = w_gate.shape[0]
    expert_count = owner_count * experts_here
    top_count = ids.shape[3]
    capacity = min(row_count, row_count * top_count // expert_count + 2)
    flat_ids = ids[0].reshape(row_count * top_count)
    onehot = (flat_ids[:, None] == jnp.arange(expert_count, dtype=jnp.int32)[None, :]).astype(
        jnp.int32
    )
    before = jnp.cumsum(onehot, axis=0) - onehot
    slot_within = jnp.sum(before * onehot, axis=1)
    slot_index = (flat_ids * capacity + slot_within).reshape(row_count, top_count)
    matching = (
        jnp.arange(expert_count * capacity, dtype=jnp.int32)[:, None, None]
        == slot_index[None, :, :]
    )
    placing = jnp.any(matching, axis=2).astype(jnp.bfloat16)
    gate_rows = gates[0].reshape(row_count, top_count).astype(jnp.float32)
    mixing = jnp.sum(jnp.where(matching, gate_rows[None, :, :], jnp.float32(0.0)), axis=2).astype(
        jnp.bfloat16
    )
    outgoing = jnp.dot(placing, normed, preferred_element_type=jnp.float32).astype(jnp.bfloat16)
    outgoing = outgoing.reshape(owner_count, experts_here, capacity, model_width)
    incoming = lax.all_to_all(outgoing, "expert", split_axis=0, concat_axis=0, tiled=True)
    gate_h = jnp.einsum("necd,edf->necf", incoming, w_gate, preferred_element_type=jnp.float32)
    up_h = jnp.einsum("necd,edf->necf", incoming, w_up, preferred_element_type=jnp.float32)
    act = (jax.nn.silu(gate_h) * up_h).astype(jnp.bfloat16)
    produced = jnp.einsum("necf,efd->necd", act, w_down, preferred_element_type=jnp.float32).astype(
        jnp.bfloat16
    )
    returned = lax.all_to_all(produced, "expert", split_axis=0, concat_axis=0, tiled=True)
    combined_rows = returned.reshape(expert_count * capacity, model_width)
    routed = jnp.einsum("st,sd->td", mixing, combined_rows, preferred_element_type=jnp.float32)
    layer_out = (residual + routed).astype(jnp.bfloat16)
    return layer_out.reshape(1, local_len, seq_count, model_width)


def solution(mesh):
    return jax.shard_map(
        shards,
        mesh=mesh,
        in_specs=(
            P("dp", "expert", None, None),
            P("dp", "expert", None, None),
            P("dp", "expert", None, None),
            P("dp", None, None, None),
            P("dp", None),
            P("dp", "expert", None, None),
            P("dp", "expert", None, None),
            P(),
            P("dp", None, None),
            P("dp", None),
            P("expert", None, None),
            P("expert", None, None),
            P("expert", None, None),
        ),
        out_specs=P("dp", "expert", None, None),
        check_vma=False,
    )
```

profile of v0, /device:TPU:32, one launch (start us, length us, event | category | flops | bytes accessed | tf_op | source)
XLA Modules:
  0.0 411.9 jit_solution(3627106416608245663)
XLA Ops:
  6.5 0.0 copy-start
  6.5 0.0 copy-start.4
  6.5 0.0 copy-start.3
  6.5 0.0 all-gather.3.cloned.1.call-start
  6.5 1.7 copy.55
  8.3 0.0 all-gather.3.cloned.1.call-update
  8.3 0.0 all-gather.5.cloned.1.call-start
  8.3 0.7 all-gather.5.cloned.1.call-update
  9.0 2.1 broadcast_in_dim.29
  11.1 4.3 %all-to-all-start = ((bf16[4,2,512,128]{3,2,1,0:T(8,128)(2,1)}), bf16[4,2,512,128]{3,2,1,0:T(8,128)(2,1)}, u32[]{:S(2)}, u32[]{:S(2)}) async-start(bf16[4,2,512,128]{3,2,1,0:T(8,128)(2,1)} %broadcast_in_dim.29), calls=%async_computation | async-start | bytes 2097152 | tf_op jit(solution)/shard_map/all_to_all | solution.py:12
  15.4 0.0 copy-start.5
  15.4 0.0 copy-done.4
  15.4 0.1 copy.60
  15.6 0.1 eq.43
  15.7 0.1 eq.39
  15.8 2.6 reshape.151
  18.4 0.7 fusion.68
  19.8 0.0 copy-done.3
  19.8 1.1 reshape.142
  21.0 1.8 reduce-window.6
  22.8 0.3 slice_reduce_fusion
  23.1 0.1 fusion.61
  23.2 0.1 reduce_sum.49
  23.3 2.5 fusion.69
  25.9 0.1 copy.59
  26.0 0.1 copy.63
  26.1 0.0 copy-done.5
  26.1 0.1 fusion.57
  26.2 2.7 convolution_bitcast_fusion
  28.9 0.4 fusion.33
  29.3 66.1 %all-gather.3.cloned.1.call-done = bf16[1,4096,2,512]{3,1,2,0:T(8,128)(2,1)} async-done(((bf16[1,64,2,512]{3,1,2,0:T(8,128)(2,1)}), bf16[1,4096,2,512]{3,1,2,0:T(8,128)(2,1)}) %all-gather.3.cloned.1.call-update) | async-done | bytes 8388624 | tf_op jit(solution)/shard_map/all_gather | solution.py:94
  95.4 38.7 %conditional.1 = ((f32[2,8,64]{2,1,0:T(8,128)S(1)}, f32[64,2,8,512]{3,0,2,1:T(8,128)})) conditional(s32[]{:T(128)} %convert_element_type.74, (f32[2,8,64]{2,1,0:T(8,128)S(1)}, f32[64,2,8,512]{3,0,2,1:T(8,128)}) %tuple.12, (s32[64]{0:T(128)S(1)}, s32[1,2]{1,0:T(1,128)}, bf16[1,4096,2,512]{3,1,2,0:T(8,128)(2,1)}, bf16[64,2,8,512]{3,2,1,0:T(8,128)(2,1)}, ...), branch_computations={%region_3.0_spmd, %region_4.7_spmd} | conditional | flops 8637918208 | bytes 75047200 | solution.py:96
  95.4 0.2 iota_compare_fusion
  95.6 0.7 iota_compare_fusion.1
  96.4 0.3 broadcast_and_fusion
  96.7 16.0 %fusion.2 = (f32[2,8,64]{2,1,0:T(8,128)}, f32[2,4096,64,8]{1,2,3,0:T(8,128)}) fusion(pred[2,64,4096]{2,1,0:T(8,128)(4,1)S(1)} %broadcast_and_fusion, bf16[64,2,8,512]{3,2,1,0:T(8,128)(2,1)} %get-tuple-element.57, bf16[1,4096,2,512]{3,1,2,0:T(8,128)(2,1)} %get-tuple-element.27), kind=kOutput, calls=%fused_computation.4 | convolution fusion | flops 4307549184 | bytes 26742784 | tf_op jit(solution)/shard_map/cond/branch_1_fun/tshl,jsl->shtj/dot_general | solution.py:74
  112.7 0.7 fusion.17
  113.4 12.4 %bitcast_add_fusion = f32[64,2,8,512]{3,0,2,1:T(8,128)} fusion(f32[64,2,8,512]{3,0,2,1:T(8,128)} %get-tuple-element.29, bf16[1,4096,2,512]{3,1,2,0:T(8,128)(2,1)} %get-tuple-element.27, f32[2,4096,64,8]{1,2,3,0:T(8,128)} %get-tuple-element.61, f32[2,8,64]{2,1,0:T(8,128)S(1)} %get-tuple-element.59, pred[2,64,4096]{2,1,0:T(8,128)(4,1)S(1)} %broadcast_and_fusion, ...), kind=kOutput, calls=%fused_computation.13 | convolution fusion | flops 4312793088 | bytes 29892608 | tf_op jit(solution)/shard_map/cond/branch_1_fun/shtj,jsl->tshl/dot_general | solution.py:85
  125.8 8.4 %fusion.1 = f32[2,8,64]{2,1,0:T(8,128)S(1)} fusion(f32[2,4096,64,8]{1,2,3,0:T(8,128)} %get-tuple-element.61, f32[2,8,64]{2,1,0:T(8,128)S(1)} %get-tuple-element.59, pred[2,64,4096]{2,1,0:T(8,128)(4,1)S(1)} %broadcast_and_fusion), kind=kLoop, calls=%fused_computation.3 | loop fusion | flops 16776192 | bytes 17309696 | tf_op jit(solution)/shard_map/cond/branch_1_fun/reduce_sum | solution.py:84
  134.1 0.0 all-to-all-done
  134.1 2.4 fusion.48
  136.6 0.2 copy.58
  136.7 8.3 %all-gather.5.cloned.1.call-done = bf16[1024,2048]{1,0:T(8,128)(2,1)} async-done(((bf16[256,2048]{1,0:T(8,128)(2,1)}), bf16[1024,2048]{1,0:T(8,128)(2,1)}) %all-gather.5.cloned.1.call-update) | async-done | bytes 4194320 | tf_op jit(solution)/shard_map/all_gather | solution.py:112
  145.1 3.3 multiply_reduce_fusion
  148.4 0.0 copy-start.1
  148.4 1.0 copy-done.1
  149.4 3.0 convolution_convert_fusion
  152.4 6.0 %reshape.134 = bf16[64,1,14,2048]{3,2,0,1:T(8,128)(2,1)} reshape(bf16[896,2048]{1,0:T(8,128)(2,1)} %convolution_convert_fusion) | data formatting | bytes 7340032 | tf_op jit(solution)/shard_map/reshape | solution.py:141
  158.4 105.4 %all_to_all.15 = bf16[64,1,14,2048]{3,2,1,0:T(8,128)(2,1)S(1)} all-to-all(bf16[64,1,14,2048]{3,2,1,0:T(8,128)(2,1)} %bitcast.151), channel_id=1, replica_groups=mesh['dp'=4,'expert'=64] {'expert'}, dimensions={0} | all-to-all | bytes 7340032 | tf_op jit(solution)/shard_map/all_to_all | solution.py:142
  263.8 1.9 copy-done.2
  265.7 0.0 copy-done.7
  265.7 8.7 %fusion.22 = f32[64,14,704]{2,0,1:T(8,128)} fusion(bf16[64,1,14,2048]{3,2,1,0:T(8,128)(2,1)S(1)} %all_to_all.15, bf16[1,2048,704]{1,2,0:T(8,128)(2,1)S(1)} %copy-done.7), kind=kOutput, calls=%fused_computation.25 | convolution fusion | flops 2583691264 | bytes 9076736 | tf_op jit(solution)/shard_map/necd,edf->necf/dot_general | solution.py:143
  274.4 0.0 copy-done
  274.4 12.9 %convert_bitcast_fusion = bf16[64,1,14,2048]{3,0,2,1:T(8,128)(2,1)} fusion(bf16[1,704,2048]{2,1,0:T(8,128)(2,1)S(1)} %copy-done, bf16[1,2048,704]{1,2,0:T(8,128)(2,1)} %param.26, bf16[64,1,14,2048]{3,2,1,0:T(8,128)(2,1)} %copy-done.2, f32[64,14,704]{2,0,1:T(8,128)} %fusion.22), kind=kOutput, calls=%fused_computation.27 | convolution fusion | flops 5173002240 | bytes 15630336 | tf_op jit(solution)/shard_map/necf,efd->necd/dot_general | solution.py:146
  287.3 6.0 %copy.68 = bf16[64,1,14,2048]{3,2,1,0:T(8,128)(2,1)} copy(bf16[64,1,14,2048]{3,0,2,1:T(8,128)(2,1)} %convert_bitcast_fusion) | data formatting | bytes 7340032 | tf_op jit(solution)/shard_map/convert_element_type | solution.py:146
  293.4 7.7 %all-to-all-start.2 = ((bf16[64,1,14,2048]{3,2,1,0:T(8,128)(2,1)}), bf16[64,1,14,2048]{3,2,1,0:T(8,128)(2,1)}, u32[]{:S(2)}, u32[]{:S(2)}) async-start(bf16[64,1,14,2048]{3,2,1,0:T(8,128)(2,1)} %copy.68), calls=%async_computation.2 | async-start | bytes 8388608 | tf_op jit(solution)/shard_map/all_to_all | solution.py:149
  301.0 0.0 copy-done.6
  301.1 0.1 copy.64
  301.2 0.1 copy.65
  301.2 1.0 select_reduce_fusion
  302.3 92.6 %all-to-all-done.2 = bf16[64,1,14,2048]{3,2,1,0:T(8,128)(2,1)} async-done(((bf16[64,1,14,2048]{3,2,1,0:T(8,128)(2,1)}), bf16[64,1,14,2048]{3,2,1,0:T(8,128)(2,1)}, u32[]{:S(2)}, u32[]{:S(2)}) %all-to-all-start.2) | async-done | bytes 3670048 | tf_op jit(solution)/shard_map/all_to_all | solution.py:149
  394.9 6.0 %reshape.140 = bf16[896,2048]{1,0:T(8,128)(2,1)} reshape(bf16[64,1,14,2048]{3,2,1,0:T(8,128)(2,1)} %all-to-all-done.2) | data formatting | bytes 7340032 | tf_op jit(solution)/shard_map/reshape | solution.py:150
  400.8 3.1 fusion.34
  404.0 1.1 reshape.141
  (11 shorter events, 0.1 us)
Async XLA Ops:
  6.5 267.9 %copy-start = (bf16[1,704,2048]{2,1,0:T(8,128)(2,1)S(1)}, bf16[1,704,2048]{2,1,0:T(8,128)(2,1)}, u32[]{:S(2)}) copy-start(bf16[1,704,2048]{2,1,0:T(8,128)(2,1)} %param.27) | copy-start | bytes 8650756
  6.5 8.9 %copy-start.4 = (s32[1,64,2,6]{1,2,3,0:T(2,128)S(1)}, s32[1,64,2,6]{1,2,3,0:T(2,128)}, u32[]{:S(2)}) copy-start(s32[1,64,2,6]{1,2,3,0:T(2,128)} %param.20) | copy-start | bytes 9220
  6.5 13.3 %copy-start.3 = (bf16[1,64,2,2048]{3,2,1,0:T(2,128)(2,1)S(1)}, bf16[1,64,2,2048]{3,2,1,0:T(2,128)(2,1)}, u32[]{:S(2)}) copy-start(bf16[1,64,2,2048]{3,2,1,0:T(2,128)(2,1)} %param.15) | copy-start | bytes 1572868
  6.5 88.9 %all-gather.3.cloned.1.call-start = ((), (), s32[]{:S(2)}) async-start(), calls=%async_computation.3 | async-start | bytes 8519680 | tf_op jit(solution)/shard_map/all_gather | solution.py:94
  8.3 136.8 %all-gather.5.cloned.1.call-start = ((), (), s32[]{:S(2)}) async-start(), calls=%async_computation.4 | async-start | bytes 5242880 | tf_op jit(solution)/shard_map/all_gather | solution.py:112
  11.1 123.0 %all-to-all-start = ((bf16[4,2,512,128]{3,2,1,0:T(8,128)(2,1)}), bf16[4,2,512,128]{3,2,1,0:T(8,128)(2,1)}, u32[]{:S(2)}, u32[]{:S(2)}) async-start(bf16[4,2,512,128]{3,2,1,0:T(8,128)(2,1)} %broadcast_in_dim.29), calls=%async_computation | async-start | bytes 2097152 | tf_op jit(solution)/shard_map/all_to_all | solution.py:12
  15.4 10.7 %copy-start.5 = (bf16[2048]{0:T(1024)(128)(2,1)S(1)}, bf16[2048]{0:T(1024)(128)(2,1)}, u32[]{:S(2)}) copy-start(bf16[2048]{0:T(1024)(128)(2,1)} %param.22) | copy-start | bytes 12292
  148.4 1.0 copy-start.1
  158.4 107.3 %copy-start.7 = (bf16[1,2048,704]{1,2,0:T(8,128)(2,1)S(1)}, bf16[1,2048,704]{1,2,0:T(8,128)(2,1)}, u32[]{:S(2)}) copy-start(bf16[1,2048,704]{1,2,0:T(8,128)(2,1)} %param.25) | copy-start | bytes 8650756
  263.8 1.9 copy-start.2
  293.4 7.7 %copy-start.6 = (bf16[1,64,2,6]{1,2,3,0:T(2,128)(2,1)S(1)}, bf16[1,64,2,6]{1,2,3,0:T(2,128)(2,1)}, u32[]{:S(2)}) copy-start(bf16[1,64,2,6]{1,2,3,0:T(2,128)(2,1)} %param.21) | copy-start | bytes 4612
  293.4 101.5 %all-to-all-start.2 = ((bf16[64,1,14,2048]{3,2,1,0:T(8,128)(2,1)}), bf16[64,1,14,2048]{3,2,1,0:T(8,128)(2,1)}, u32[]{:S(2)}, u32[]{:S(2)}) async-start(bf16[64,1,14,2048]{3,2,1,0:T(8,128)(2,1)} %copy.68), calls=%async_computation.2 | async-start | bytes 8388608 | tf_op jit(solution)/shard_map/all_to_all | solution.py:149
Sparse Core Ops, SparseCore 0:
  10.1 85.2 all-gather.2
  97.2 47.8 all-gather.4
where the time goes:
time: 416 us; the launch traced here: 412 us
  waiting for transfers between devices  168 us (40%)
  blocking collectives  105 us (25%)
  matrix products  67.1 us (16%)
  local copies, waits for them, and re-layouts  30.9 us (7%)
  other arithmetic  14.6 us (4%)
  between operations  14.2 us (3%)
  starting transfers between devices  12 us (3%)
    all_to_all x1, blocking collectives, shards(): lax.all_to_all(outgoing, 'expert', split_axis=0, concat_axis=0, tiled=True)  105 us
    all_to_all x1, waiting for transfers between devices, shards(): lax.all_to_all(produced, 'expert', split_axis=0, concat_axis=0, tiled=True)  92.6 us
    all_gather x1, waiting for transfers between devices, shards(): portion = lax.all_gather(latents, 'expert', axis=1, tiled=True)  66.1 us
    dot_general x1, matrix products, fold_step(): jnp.einsum('tshl,jsl->shtj', query_rows, key_rows, preferred_element_type...  16 us
    dot_general x1, matrix products, shards(): jnp.einsum('necf,efd->necd', act, w_down, preferred_element_type=jnp.floa...  12.9 us
    dot_general x1, matrix products, fold_step(): jnp.einsum('shtj,jsl->tshl', weights.astype(jnp.bfloat16), key_rows, pref...  12.4 us
    dot_general x1, matrix products, shards(): jnp.einsum('necd,edf->necf', incoming, w_gate, preferred_element_type=jnp...  8.67 us
    reduce_sum x1, other arithmetic, fold_step(): new_sum = old_sum * factor + jnp.sum(weights, axis=3)  8.36 us
  transfers between devices with their start and end apart: 4, of which 3 were waited for; matrix products, arithmetic and copies ran while one was open for 14% of the time, Pallas kernels for 0%

commit v1 on v0

--- a/solution.py
+++ b/solution.py
@@ -1,10 +1,390 @@
 import jax
 import jax.numpy as jnp
 from jax import lax
+from jax.experimental import pallas as pl
+from jax.experimental.pallas import tpu as pltpu
 from jax.sharding import PartitionSpec as P
 
 score_scale = 192.0 ** (-0.5)
 norm_eps = 1e-06
+NY, NZ, NC = 4, 8, 2
+Q = 8
+TOK = 128
+CAP = 14
+EXPERTS = 64
+PEERS = NY * NC
+ROWS = NZ * CAP
+ALLROWS = PEERS * ROWS
+
+
+def place():
+    me = lax.axis_index("expert")
+    c = lax.rem(me, NC)
+    z = lax.rem(lax.div(me, NC), NZ)
+    y = lax.div(me, NC * NZ)
+    return me, y, z, c
+
+
+def device_at(y, z, c):
+    return (y * NZ + z) * NC + c
+
+
+def wrap(v, n):
+    return lax.rem(v + 2 * n, n)
+
+
+def send(src, dst, ssem, rsem, to):
+    return pltpu.make_async_remote_copy(
+        src_ref=src,
+        dst_ref=dst,
+        send_sem=ssem,
+        recv_sem=rsem,
+        device_id={"expert": to},
+        device_id_type=pl.DeviceIdType.MESH,
+    )
+
+
+def bdot(a, b):
+    return jnp.dot(a, b, preferred_element_type=jnp.float32)
+
+
+def expert_kernel(
+    nq_hbm, resid_hbm, ids_ref, gates_ref, wg_hbm, wu_hbm, wd_hbm, out_ref,
+    xs, place_m, mix_m, sent, got, gate_acc, up_acc, act, wg, wu, wd, back, part, landed, resid, table,
+    load_sem, zsend, zrecv, ysend, yrecv, osend, orecv, rsend, rrecv, tsend, trecv,
+):
+    width = xs.shape[3]
+    me, y, z, c = place()
+    my_slot = y * NC + c
+
+    loads = [
+        pltpu.make_async_copy(nq_hbm, xs.at[z], load_sem.at[0]),
+        pltpu.make_async_copy(wg_hbm, wg, load_sem.at[1]),
+        pltpu.make_async_copy(wu_hbm, wu, load_sem.at[2]),
+        pltpu.make_async_copy(wd_hbm, wd, load_sem.at[3]),
+        pltpu.make_async_copy(resid_hbm, resid, load_sem.at[4]),
+    ]
+    for load in loads:
+        load.start()
+
+    barrier = pltpu.get_barrier_semaphore()
+    partners = []
+    for k in range(1, PEERS):
+        slot = wrap(my_slot + k, PEERS)
+        partners.append(device_at(lax.div(slot, NC), z, lax.rem(slot, NC)))
+    around = [device_at(y, wrap(z + 1, NZ), c), device_at(y, wrap(z - 1, NZ), c)]
+    for dev in partners + around:
+        pl.semaphore_signal(barrier, inc=1, device_id={"expert": dev}, device_id_type=pl.DeviceIdType.MESH)
+
+    expert_iota = lax.broadcasted_iota(jnp.int32, (EXPERTS, TOK), 0)
+    hits = []
+    named = jnp.zeros((EXPERTS, TOK), jnp.float32)
+    for k in range(6):
+        hit = expert_iota == jnp.broadcast_to(ids_ref[k : k + 1, :], (EXPERTS, TOK))
+        hits.append(hit)
+        named = named + jnp.where(hit, 1.0, 0.0)
+    earlier = lax.broadcasted_iota(jnp.int32, (TOK, TOK), 0) < lax.broadcasted_iota(jnp.int32, (TOK, TOK), 1)
+    before = bdot(named.astype(jnp.bfloat16), jnp.where(earlier, 1.0, 0.0).astype(jnp.bfloat16))
+    expert_base = (expert_iota * CAP + z * (EXPERTS * CAP)).astype(jnp.float32)
+    rows = []
+    for k in range(6):
+        rows.append(jnp.sum(jnp.where(hits[k], before + expert_base, 0.0), axis=0, keepdims=True))
+    filler = jnp.full((2, TOK), -1.0, jnp.float32)
+    table[z] = jnp.concatenate(rows + [filler, gates_ref[...]], axis=0)
+
+    pl.semaphore_wait(barrier, len(partners) + len(around))
+    loads[0].wait()
+
+    def z_copy(block, j, sem_slot, to):
+        return send(xs.at[block, j], xs.at[block, j], zsend.at[j, sem_slot], zrecv.at[j, block], to)
+
+    def t_copy(block, sem_slot, to):
+        return send(table.at[block], table.at[block], tsend.at[sem_slot], trecv.at[block], to)
+
+    def y_copy(k, j):
+        slot = wrap(my_slot + k, PEERS)
+        to = device_at(lax.div(slot, NC), z, lax.rem(slot, NC))
+        return send(sent.at[j, slot], got.at[j, my_slot], ysend.at[j, k], yrecv.at[j, my_slot], to)
+
+    def wait_y(k, j):
+        slot = wrap(my_slot + k, PEERS)
+        to = device_at(lax.div(slot, NC), z, lax.rem(slot, NC))
+        send(sent.at[j, slot], got.at[j, slot], ysend.at[j, k], yrecv.at[j, slot], to).wait_recv()
+
+    def o_copy(k, j):
+        slot = wrap(my_slot + k, PEERS)
+        to = device_at(lax.div(slot, NC), z, lax.rem(slot, NC))
+        return send(sent.at[j, slot], back.at[j, my_slot], osend.at[j, k], orecv.at[j, my_slot], to)
+
+    def wait_o(k, j):
+        slot = wrap(my_slot + k, PEERS)
+        to = device_at(lax.div(slot, NC), z, lax.rem(slot, NC))
+        send(sent.at[j, slot], back.at[j, slot], osend.at[j, k], orecv.at[j, slot], to).wait_recv()
+
+    def direction(j):
+        return 1 - 2 * lax.rem(j, 2)
+
+    def z_major(j, s):
+        d = direction(j)
+        return z_copy(wrap(z - d * s, NZ), j, s, device_at(y, wrap(z + d, NZ), c))
+
+    def z_minor(j, s):
+        d = direction(j)
+        return z_copy(wrap(z + d * s, NZ), j, 4 + s, device_at(y, wrap(z - d, NZ), c))
+
+    def t_major(s):
+        return t_copy(wrap(z - s, NZ), s, device_at(y, wrap(z + 1, NZ), c))
+
+    def t_minor(s):
+        return t_copy(wrap(z + s, NZ), 4 + s, device_at(y, wrap(z - 1, NZ), c))
+
+    def build_tables():
+        r = lax.broadcasted_iota(jnp.int32, (ALLROWS, TOK), 0)
+        group = lax.shift_right_logical(r * 9363, 17)
+        within = r - group * CAP
+        peer = lax.shift_right_logical(group, 3)
+        block = group - peer * NZ
+        owner_y = lax.shift_right_logical(peer, 1)
+        owner_c = peer - owner_y * NC
+        owner = (owner_y * NZ + z) * NC + owner_c
+        code = (block * (EXPERTS * CAP) + owner * CAP + within).astype(jnp.float32)
+
+        def one_block(b, carry):
+            rows_b = table[b]
+            hot = jnp.zeros((ALLROWS, TOK), jnp.float32)
+            mixed = jnp.zeros((ALLROWS, TOK), jnp.float32)
+            for k in range(6):
+                hit = code == jnp.broadcast_to(rows_b[k : k + 1, :], (ALLROWS, TOK))
+                hot = jnp.where(hit, 1.0, hot)
+                mixed = jnp.where(hit, jnp.broadcast_to(rows_b[8 + k : 9 + k, :], (ALLROWS, TOK)), mixed)
+            place_m[:, pl.ds(pl.multiple_of(b * TOK, TOK), TOK)] = hot.astype(jnp.bfloat16)
+            mix_m[b] = mixed.T.astype(jnp.bfloat16)
+            return carry
+
+        lax.fori_loop(0, NZ, one_block, 0)
+
+    gate_acc[...] = jnp.zeros_like(gate_acc)
+    up_acc[...] = jnp.zeros_like(up_acc)
+
+    def dispatch_step(i, carry):
+        for s in range(4):
+            j = i - s
+
+            @pl.when((j >= 0) & (j < Q))
+            def _():
+                d = direction(j)
+                block = wrap(z - d * s, NZ)
+                copy = z_major(j, s)
+                if s > 0:
+                    z_copy(block, j, s, device_at(y, wrap(z + d, NZ), c)).wait_recv()
+                copy.start()
+                if s < 3:
+                    block2 = wrap(z + d * s, NZ)
+                    copy2 = z_minor(j, s)
+                    if s > 0:
+                        z_copy(block2, j, 4 + s, device_at(y, wrap(z - d, NZ), c)).wait_recv()
+                    copy2.start()
+
+        for s in range(4):
+
+            @pl.when(i == s)
+            def _():
+                copy = t_major(s)
+                if s > 0:
+                    copy.wait_recv()
+                copy.start()
+                if s < 3:
+                    copy2 = t_minor(s)
+                    if s > 0:
+                        copy2.wait_recv()
+                    copy2.start()
+
+        @pl.when(i == 4)
+        def _():
+            t_copy(wrap(z - 4, NZ), 0, me).wait_recv()
+            t_copy(wrap(z + 3, NZ), 0, me).wait_recv()
+            build_tables()
+
+        j = i - 4
+
+        @pl.when((j >= 0) & (j < Q))
+        def _():
+            d = direction(j)
+            z_copy(wrap(z - 4 * d, NZ), j, 0, me).wait_recv()
+            z_copy(wrap(z + 3 * d, NZ), j, 0, me).wait_recv()
+            block_rows = xs[:, j].reshape(NZ * TOK, width)
+            packed = bdot(place_m[...], block_rows).astype(jnp.bfloat16)
+            sent[j] = packed.reshape(PEERS, ROWS, width)
+            got[j, my_slot] = sent[j, my_slot]
+
+        j2 = i - 6
+
+        @pl.when(j2 >= 0)
+        def _():
+            @pl.when(j2 == 0)
+            def _():
+                loads[1].wait()
+                loads[2].wait()
+
+            for k in range(1, PEERS):
+                wait_y(k, j2)
+            x = got[j2].reshape(ALLROWS, width)
+            cols = pl.ds(pl.multiple_of(j2 * width, width), width)
+            gate_acc[...] += bdot(x, wg[cols, :])
+            up_acc[...] += bdot(x, wu[cols, :])
+
+        @pl.when((j >= 0) & (j < Q))
+        def _():
+            for k in range(1, PEERS):
+                y_copy(k, j).start()
+
+        return carry
+
+    lax.fori_loop(0, Q + 6, dispatch_step, 0)
+
+    g = gate_acc[...]
+    act[...] = ((g / (1.0 + jnp.exp(-g))) * up_acc[...]).astype(jnp.bfloat16)
+    loads[3].wait()
+    loads[4].wait()
+
+    def drain_dispatch(j, carry):
+        for s in range(4):
+            z_major(j, s).wait_send()
+            if s < 3:
+                z_minor(j, s).wait_send()
+        for k in range(1, PEERS):
+            y_copy(k, j).wait_send()
+        return carry
+
+    lax.fori_loop(0, Q, drain_dispatch, 0)
+    for s in range(4):
+        t_major(s).wait_send()
+        if s < 3:
+            t_minor(s).wait_send()
+
+    def r_major(j, s):
+        return send(xs.at[s, j], landed.at[s, j], rsend.at[j, s], rrecv.at[j, s],
+                    device_at(y, wrap(z + direction(j), NZ), c))
+
+    def r_minor(j, s):
+        return send(xs.at[4 + s, j], landed.at[4 + s, j], rsend.at[j, 4 + s], rrecv.at[j, 4 + s],
+                    device_at(y, wrap(z - direction(j), NZ), c))
+
+    def combine_step(i, carry):
+        @pl.when(i < Q)
+        def _():
+            cols = pl.ds(pl.multiple_of(i * width, width), width)
+            made = bdot(act[...], wd[:, cols]).astype(jnp.bfloat16)
+            sent[i] = made.reshape(PEERS, ROWS, width)
+            back[i, my_slot] = sent[i, my_slot]
+
+        jm = i - 2
+
+        @pl.when((jm >= 0) & (jm < Q))
+        def _():
+            for k in range(1, PEERS):
+                wait_o(k, jm)
+            rows_in = back[jm].reshape(ALLROWS, width)
+            mixed = bdot(mix_m[...].reshape(NZ * TOK, ALLROWS), rows_in)
+            part[jm] = mixed.reshape(NZ, TOK, width)
+
+        for s in (3, 2, 1, 0):
+            j = i - 2 - s
+
+            @pl.when((j >= 0) & (j < Q))
+            def _():
+                d = direction(j)
+                value = part[j, wrap(z + d * (4 - s), NZ)]
+                if s > 0:
+                    r_major(j, s - 1).wait_recv()
+                    value = value + landed[s - 1, j].astype(jnp.float32)
+                xs[s, j] = value.astype(jnp.bfloat16)
+                if s < 3:
+                    value2 = part[j, wrap(z - d * (3 - s), NZ)]
+                    if s > 0:
+                        r_minor(j, s - 1).wait_recv()
+                        value2 = value2 + landed[4 + s - 1, j].astype(jnp.float32)
+                    xs[4 + s, j] = value2.astype(jnp.bfloat16)
+
+        for s in (3, 2, 1, 0):
+            j = i - 2 - s
+
+            @pl.when((j >= 0) & (j < Q))
+            def _():
+                r_major(j, s).start()
+                if s < 3:
+                    r_minor(j, s).start()
+
+        @pl.when(i < Q)
+        def _():
+            for k in range(1, PEERS):
+                o_copy(k, i).start()
+
+        jf = i - 6
+
+        @pl.when((jf >= 0) & (jf < Q))
+        def _():
+            r_major(jf, 3).wait_recv()
+            r_minor(jf, 2).wait_recv()
+            total = part[jf, z] + landed[3, jf].astype(jnp.float32) + landed[6, jf].astype(jnp.float32)
+            cols = pl.ds(pl.multiple_of(jf * width, width), width)
+            out_ref[:, cols] = (resid[:, cols] + total).astype(jnp.bfloat16)
+
+        return carry
+
+    lax.fori_loop(0, Q + 6, combine_step, 0)
+
+    def drain_combine(j, carry):
+        for s in range(4):
+            r_major(j, s).wait_send()
+            if s < 3:
+                r_minor(j, s).wait_send()
+        for k in range(1, PEERS):
+            o_copy(k, j).wait_send()
+        return carry
+
+    lax.fori_loop(0, Q, drain_combine, 0)
+
+
+def run_experts(nq, resid, ids_t, gates_t, w_gate, w_up, w_down):
+    width = nq.shape[2]
+    model_width = w_gate.shape[0]
+    hidden_units = w_gate.shape[1]
+    anywhere = pl.BlockSpec(memory_space=pl.ANY)
+    vmem = pl.BlockSpec(memory_space=pltpu.VMEM)
+    bf16, f32 = jnp.bfloat16, jnp.float32
+    dma = pltpu.SemaphoreType.DMA
+    return pl.pallas_call(
+        expert_kernel,
+        out_shape=jax.ShapeDtypeStruct((TOK, model_width), bf16),
+        in_specs=[anywhere, anywhere, vmem, vmem, anywhere, anywhere, anywhere],
+        out_specs=vmem,
+        scratch_shapes=[
+            pltpu.VMEM((NZ, Q, TOK, width), bf16),
+            pltpu.VMEM((ALLROWS, NZ * TOK), bf16),
+            pltpu.VMEM((NZ, TOK, ALLROWS), bf16),
+            pltpu.VMEM((Q, PEERS, ROWS, width), bf16),
+            pltpu.VMEM((Q, PEERS, ROWS, width), bf16),
+            pltpu.VMEM((ALLROWS, hidden_units), f32),
+            pltpu.VMEM((ALLROWS, hidden_units), f32),
+            pltpu.VMEM((ALLROWS, hidden_units), bf16),
+            pltpu.VMEM((model_width, hidden_units), bf16),
+            pltpu.VMEM((model_width, hidden_units), bf16),
+            pltpu.VMEM((hidden_units, model_width), bf16),
+            pltpu.VMEM((Q, PEERS, ROWS, width), bf16),
+            pltpu.VMEM((Q, NZ, TOK, width), f32),
+            pltpu.VMEM((7, Q, TOK, width), bf16),
+            pltpu.VMEM((TOK, model_width), f32),
+            pltpu.VMEM((NZ, 16, TOK), f32),
+            dma((5,)),
+            dma((Q, 7)), dma((Q, NZ)), dma((Q, PEERS)), dma((Q, PEERS)), dma((Q, PEERS)), dma((Q, PEERS)),
+            dma((Q, 7)), dma((Q, 7)), dma((7,)), dma((NZ,)),
+        ],
+        compiler_params=pltpu.CompilerParams(
+            collective_id=1, has_side_effects=True, vmem_limit_bytes=60 * 1024 * 1024
+        ),
+        name="experts",
+    )(nq, resid, ids_t, gates_t, w_gate, w_up, w_down)
 
 
 def sent_to_all(shard, axis):
@@ -117,39 +497,11 @@
     normed = (residual * lax.rsqrt(mean_square + norm_eps) * norm_gain.astype(jnp.float32)).astype(
         jnp.bfloat16
     )
-    experts_here = w_gate.shape[0]
-    expert_count = owner_count * experts_here
-    top_count = ids.shape[3]
-    capacity = min(row_count, row_count * top_count // expert_count + 2)
-    flat_ids = ids[0].reshape(row_count * top_count)
-    onehot = (flat_ids[:, None] == jnp.arange(expert_count, dtype=jnp.int32)[None, :]).astype(
-        jnp.int32
-    )
-    before = jnp.cumsum(onehot, axis=0) - onehot
-    slot_within = jnp.sum(before * onehot, axis=1)
-    slot_index = (flat_ids * capacity + slot_within).reshape(row_count, top_count)
-    matching = (
-        jnp.arange(expert_count * capacity, dtype=jnp.int32)[:, None, None]
-        == slot_index[None, :, :]
-    )
-    placing = jnp.any(matching, axis=2).astype(jnp.bfloat16)
-    gate_rows = gates[0].reshape(row_count, top_count).astype(jnp.float32)
-    mixing = jnp.sum(jnp.where(matching, gate_rows[None, :, :], jnp.float32(0.0)), axis=2).astype(
-        jnp.bfloat16
-    )
-    outgoing = jnp.dot(placing, normed, preferred_element_type=jnp.float32).astype(jnp.bfloat16)
-    outgoing = outgoing.reshape(owner_count, experts_here, capacity, model_width)
-    incoming = lax.all_to_all(outgoing, "expert", split_axis=0, concat_axis=0, tiled=True)
-    gate_h = jnp.einsum("necd,edf->necf", incoming, w_gate, preferred_element_type=jnp.float32)
-    up_h = jnp.einsum("necd,edf->necf", incoming, w_up, preferred_element_type=jnp.float32)
-    act = (jax.nn.silu(gate_h) * up_h).astype(jnp.bfloat16)
-    produced = jnp.einsum("necf,efd->necd", act, w_down, preferred_element_type=jnp.float32).astype(
-        jnp.bfloat16
-    )
-    returned = lax.all_to_all(produced, "expert", split_axis=0, concat_axis=0, tiled=True)
-    combined_rows = returned.reshape(expert_count * capacity, model_width)
-    routed = jnp.einsum("st,sd->td", mixing, combined_rows, preferred_element_type=jnp.float32)
-    layer_out = (residual + routed).astype(jnp.bfloat16)
+    width = model_width // Q
+    nq = jnp.moveaxis(normed.reshape(row_count, Q, width), 1, 0)
+    ids_t = jnp.pad(ids[0].reshape(row_count, -1).T, ((0, 2), (0, 0)), constant_values=-1)
+    gates_t = jnp.pad(gates[0].reshape(row_count, -1).T.astype(jnp.float32), ((0, 2), (0, 0)))
+    layer_out = run_experts(nq, residual, ids_t, gates_t, w_gate[0], w_up[0], w_down[0])
     return layer_out.reshape(1, local_len, seq_count, model_width)
 
 

time: 416 us -> 313 us (0.75)
  Pallas kernels: 0 us -> 154 us
  blocking collectives: 105 us -> 0 us
  waiting for transfers between devices: 168 us -> 69.6 us
  matrix products: 67.1 us -> 37.7 us
  local copies, waits for them, and re-layouts: 30.9 us -> 23.1 us
  starting transfers between devices: 12 us -> 4.34 us
  other arithmetic: 14.6 us -> 9.45 us
    pallas_call x0 -> x1, Pallas kernels: none -> 154 us  [run_experts(): pl.pallas_call(expert_kernel, out_shape=jax.ShapeDtypeStruct((TOK, model_...]
    all_to_all x1 -> x0, blocking collectives: 105 us -> none  [shards(): lax.all_to_all(outgoing, 'expert', split_axis=0, concat_axis=0, tiled=True)]
    all_to_all x1 -> x0, waiting for transfers between devices: 92.6 us -> none  [shards(): lax.all_to_all(produced, 'expert', split_axis=0, concat_axis=0, tiled=True)]
    dot_general x4 -> x0, matrix products: 27.8 us -> none  [the longest x1 12.9 us: shards(): jnp.einsum('necf,efd->necd', act, w_down, preferred_element_type=jnp.floa...]
    reshape x2 -> x1, local copies, waits for them, and re-layouts: 12 us -> 0.96 us  [shards(): nq = jnp.moveaxis(normed.reshape(row_count, Q, width), 1, 0)]
    all_to_all x1 -> x0, starting transfers between devices: 7.67 us -> none  [shards(): lax.all_to_all(produced, 'expert', split_axis=0, concat_axis=0, tiled=True)]
    all_gather x1, waiting for transfers between devices: 66.1 us -> 59 us  [shards(): portion = lax.all_gather(latents, 'expert', axis=1, tiled=True)]
    unnamed x18 -> x17, local copies, waits for them, and re-layouts: 4.77 us -> 11.2 us
  transfers between devices with their start and end apart: 4 -> 3, of which waited for: 3 -> 2; matrix products, arithmetic and copies ran while one was open for 14% -> 19% of each run, Pallas kernels for 0% -> 0%
where the time goes in v1:
time: 313 us; the launch traced here: 312 us
  Pallas kernels  154 us (49%)
  waiting for transfers between devices  69.6 us (22%)
  matrix products  37.7 us (12%)
  local copies, waits for them, and re-layouts  23.1 us (7%)
  between operations  14.1 us (5%)
  other arithmetic  9.45 us (3%)
  starting transfers between devices  4.34 us (1%)
    pallas_call x1, Pallas kernels, run_experts(): pl.pallas_call(expert_kernel, out_shape=jax.ShapeDtypeStruct((TOK, model_...  154 us
    all_gather x1, waiting for transfers between devices, shards(): portion = lax.all_gather(latents, 'expert', axis=1, tiled=True)  59 us
    dot_general x1, matrix products, fold_step(): jnp.einsum('tshl,jsl->shtj', query_rows, key_rows, preferred_element_type...  15.6 us
    dot_general x1, matrix products, fold_step(): jnp.einsum('shtj,jsl->tshl', weights.astype(jnp.bfloat16), key_rows, pref...  12.6 us
    unnamed x17, local copies, waits for them, and re-layouts  11.2 us
    all_gather x1, waiting for transfers between devices, shards(): lax.all_gather(w_out, 'dp', axis=0, tiled=True)  9.83 us
  transfers between devices with their start and end apart: 3, of which 2 were waited for; matrix products, arithmetic and copies ran while one was open for 19% of the time, Pallas kernels for 0%

profile of v1, /device:TPU:32, one launch (start us, length us, event | category | flops | bytes accessed | tf_op | source)
XLA Modules:
  0.0 312.5 jit_solution(6183581290539290666)
XLA Ops:
  6.5 0.0 copy-start.4
  6.5 0.0 all-gather.3.cloned.1.call-start
  6.5 1.6 copy.28
  8.1 0.0 all-gather.3.cloned.1.call-update
  8.1 0.0 all-gather.5.cloned.1.call-start
  8.2 0.7 all-gather.5.cloned.1.call-update
  8.9 2.0 broadcast_in_dim.14
  10.9 4.3 %all-to-all-start = ((bf16[4,2,512,128]{3,2,1,0:T(8,128)(2,1)}), bf16[4,2,512,128]{3,2,1,0:T(8,128)(2,1)S(1)}, u32[]{:S(2)}, u32[]{:S(2)}) async-start(bf16[4,2,512,128]{3,2,1,0:T(8,128)(2,1)} %broadcast_in_dim.14), calls=%async_computation | async-start | bytes 2097152 | tf_op jit(solution)/shard_map/all_to_all | solution.py:392
  15.2 0.0 copy-start.3
  15.2 0.0 copy-start.5
  15.2 0.0 copy-start.2
  15.2 2.6 reshape.83
  17.9 0.7 fusion.32
  19.2 1.2 reshape.78
  20.4 0.0 copy-done.4
  20.4 0.0 copy-start.6
  20.4 4.7 %copy.37 = bf16[1,2048,704]{2,1,0:T(8,128)(2,1)} copy(bf16[1,2048,704]{1,2,0:T(8,128)(2,1)} %param.25) | data formatting | bytes 5767168 | tf_op args[10]
  25.1 4.7 %copy.38 = bf16[1,2048,704]{2,1,0:T(8,128)(2,1)} copy(bf16[1,2048,704]{1,2,0:T(8,128)(2,1)} %param.26) | data formatting | bytes 5767168 | tf_op args[11]
  29.7 0.0 copy-done.3
  29.7 0.1 copy.33
  29.8 0.1 copy.34
  29.9 0.0 copy-done.5
  29.9 0.1 copy.35
  30.0 0.1 copy.36
  30.1 0.0 copy-done.2
  30.1 2.6 fusion.33
  32.7 0.7 fusion.27
  33.3 1.9 convolution_bitcast_fusion
  35.2 0.6 pad.10.ids_ref
  35.8 0.6 pad_convert_fusion.gates_ref
  36.4 59.0 %all-gather.3.cloned.1.call-done = bf16[1,4096,2,512]{3,1,2,0:T(8,128)(2,1)} async-done(((bf16[1,64,2,512]{3,1,2,0:T(8,128)(2,1)}), bf16[1,4096,2,512]{3,1,2,0:T(8,128)(2,1)}) %all-gather.3.cloned.1.call-update) | async-done | bytes 8388624 | tf_op jit(solution)/shard_map/all_gather | solution.py:474
  95.4 0.0 copy-done.6
  95.4 37.5 %conditional.1 = ((f32[2,8,64]{2,1,0:T(8,128)}, f32[64,2,8,512]{3,0,2,1:T(8,128)})) conditional(s32[]{:T(128)} %convert_element_type.41, (f32[2,8,64]{2,1,0:T(8,128)}, f32[64,2,8,512]{3,0,2,1:T(8,128)}) %tuple.12, (s32[64]{0:T(128)S(1)}, s32[1,2]{1,0:T(1,128)S(1)}, bf16[1,4096,2,512]{3,1,2,0:T(8,128)(2,1)}, bf16[64,2,8,512]{3,2,1,0:T(8,128)(2,1)}, ...), branch_computations={%region_3.0_spmd, %region_4.7_spmd} | conditional | flops 8637918208 | bytes 142156096 | solution.py:476
  95.4 0.2 iota_compare_fusion
  95.6 0.1 iota_compare_fusion.1
  95.7 0.3 broadcast_and_fusion
  96.0 15.6 %fusion.2 = (f32[2,8,64]{2,1,0:T(8,128)S(1)}, f32[2,4096,64,8]{1,2,3,0:T(8,128)}) fusion(pred[2,64,4096]{2,1,0:T(8,128)(4,1)S(1)} %broadcast_and_fusion, bf16[64,2,8,512]{3,2,1,0:T(8,128)(2,1)} %get-tuple-element.43, bf16[1,4096,2,512]{3,1,2,0:T(8,128)(2,1)} %get-tuple-element.27), kind=kOutput, calls=%fused_computation.4 | convolution fusion | flops 4307549184 | bytes 26742784 | tf_op jit(solution)/shard_map/cond/branch_1_fun/tshl,jsl->shtj/dot_general | solution.py:454
  111.6 0.6 fusion.17
  112.2 0.0 copy-start
  112.2 12.6 %bitcast_add_fusion = f32[64,2,8,512]{3,0,2,1:T(8,128)} fusion(f32[64,2,8,512]{3,0,2,1:T(8,128)} %get-tuple-element.29, bf16[1,4096,2,512]{3,1,2,0:T(8,128)(2,1)} %get-tuple-element.27, f32[2,4096,64,8]{1,2,3,0:T(8,128)} %get-tuple-element.47, f32[2,8,64]{2,1,0:T(8,128)S(1)} %get-tuple-element.45, pred[2,64,4096]{2,1,0:T(8,128)(4,1)S(1)} %broadcast_and_fusion, ...), kind=kOutput, calls=%fused_computation.13 | convolution fusion | flops 4312793088 | bytes 29892608 | tf_op jit(solution)/shard_map/cond/branch_1_fun/shtj,jsl->tshl/dot_general | solution.py:465
  124.8 2.0 copy-done
  126.8 4.8 %fusion.1 = f32[2,8,64]{2,1,0:T(8,128)S(1)} fusion(f32[2,4096,64,8]{1,2,3,0:T(8,128)S(1)} %copy-done, f32[2,8,64]{2,1,0:T(8,128)S(1)} %get-tuple-element.45, pred[2,64,4096]{2,1,0:T(8,128)(4,1)S(1)} %broadcast_and_fusion), kind=kLoop, calls=%fused_computation.3 | loop fusion | flops 16776192 | bytes 17309696 | tf_op jit(solution)/shard_map/cond/branch_1_fun/reduce_sum | solution.py:464
  131.7 1.3 multiply_add_fusion
  133.0 0.0 all-to-all-done
  133.0 2.1 fusion.20
  135.1 0.2 copy.31
  135.2 9.8 %all-gather.5.cloned.1.call-done = bf16[1024,2048]{1,0:T(8,128)(2,1)} async-done(((bf16[256,2048]{1,0:T(8,128)(2,1)}), bf16[1024,2048]{1,0:T(8,128)(2,1)}) %all-gather.5.cloned.1.call-update) | async-done | bytes 4194320 | tf_op jit(solution)/shard_map/all_gather | solution.py:492
  145.1 3.0 multiply_reduce_fusion
  148.1 0.0 copy-start.1
  148.1 0.2 multiply_convert_fusion
  148.3 1.0 copy.76
  149.3 0.0 copy-done.1
  149.3 154.2 %experts.1 = bf16[128,2048]{1,0:T(8,128)(2,1)} custom-call(bf16[8,128,256]{2,1,0:T(8,128)(2,1)} %bitcast.70, f32[128,2048]{1,0:T(8,128)} %copy-done.1, s32[8,128]{1,0:T(8,128)} %pad.10.ids_ref, f32[8,128]{1,0:T(8,128)} %pad_convert_fusion.gates_ref, bf16[2048,704]{1,0:T(8,128)(2,1)} %bitcast.67, bf16[2048,704]{1,0:T(8,128)(2,1)} %bitcast.68, ...), custom_call_target="tpu_custom_call" | custom-call | tf_op jit(solution)/shard_map/experts/pallas_call | solution.py:357
  303.4 2.2 reshape.77
  (3 shorter events, 0.0 us)
Async XLA Ops:
  6.5 13.8 %copy-start.4 = (bf16[2048]{0:T(1024)(128)(2,1)S(1)}, bf16[2048]{0:T(1024)(128)(2,1)}, u32[]{:S(2)}) copy-start(bf16[2048]{0:T(1024)(128)(2,1)} %param.22) | copy-start | bytes 12292
  6.5 88.9 %all-gather.3.cloned.1.call-start = ((), (), s32[]{:S(2)}) async-start(), calls=%async_computation.1 | async-start | bytes 8519680 | tf_op jit(solution)/shard_map/all_gather | solution.py:474
  8.1 136.9 %all-gather.5.cloned.1.call-start = ((), (), s32[]{:S(2)}) async-start(), calls=%async_computation.2 | async-start | bytes 5242880 | tf_op jit(solution)/shard_map/all_gather | solution.py:492
  10.9 122.0 %all-to-all-start = ((bf16[4,2,512,128]{3,2,1,0:T(8,128)(2,1)}), bf16[4,2,512,128]{3,2,1,0:T(8,128)(2,1)S(1)}, u32[]{:S(2)}, u32[]{:S(2)}) async-start(bf16[4,2,512,128]{3,2,1,0:T(8,128)(2,1)} %broadcast_in_dim.14), calls=%async_computation | async-start | bytes 2097152 | tf_op jit(solution)/shard_map/all_to_all | solution.py:392
  15.2 14.5 %copy-start.3 = (s32[1,64,2,6]{1,2,3,0:T(2,128)S(1)}, s32[1,64,2,6]{1,2,3,0:T(2,128)}, u32[]{:S(2)}) copy-start(s32[1,64,2,6]{1,2,3,0:T(2,128)} %param.20) | copy-start | bytes 9220
  15.2 14.7 %copy-start.5 = (bf16[1,64,2,6]{1,2,3,0:T(2,128)(2,1)S(1)}, bf16[1,64,2,6]{1,2,3,0:T(2,128)(2,1)}, u32[]{:S(2)}) copy-start(bf16[1,64,2,6]{1,2,3,0:T(2,128)(2,1)} %param.21) | copy-start | bytes 4612
  15.2 14.9 %copy-start.2 = (bf16[1,32,2,512]{3,2,1,0:T(2,128)(2,1)S(1)}, bf16[1,32,2,512]{3,2,1,0:T(2,128)(2,1)}, u32[]{:S(2)}) copy-start(bf16[1,32,2,512]{3,2,1,0:T(2,128)(2,1)} %param.18) | copy-start | bytes 196612
  20.4 75.0 %copy-start.6 = (s32[1,2]{1,0:T(1,128)S(1)}, s32[1,2]{1,0:T(1,128)}, u32[]{:S(2)}) copy-start(s32[1,2]{1,0:T(1,128)} %param.19) | copy-start | bytes 28
  112.2 14.6 %copy-start = (f32[2,4096,64,8]{1,2,3,0:T(8,128)S(1)}, f32[2,4096,64,8]{1,2,3,0:T(8,128)}, u32[]{:S(2)}) copy-start(f32[2,4096,64,8]{1,2,3,0:T(8,128)} %get-tuple-element.47) | copy-start | bytes 50331652 | tf_op jit(solution)/shard_map/cond
  148.1 1.1 copy-start.1
Sparse Core Ops, SparseCore 0:
  10.1 85.2 all-gather.2
  97.2 47.8 all-gather.4

commit v2 on v1

--- a/solution.py
+++ b/solution.py
@@ -7,6 +7,8 @@
 
 score_scale = 192.0 ** (-0.5)
 norm_eps = 1e-06
+
+
 NY, NZ, NC = 4, 8, 2
 Q = 8
 TOK = 128
@@ -230,8 +232,8 @@
                 wait_y(k, j2)
             x = got[j2].reshape(ALLROWS, width)
             cols = pl.ds(pl.multiple_of(j2 * width, width), width)
-            gate_acc[...] += bdot(x, wg[cols, :])
-            up_acc[...] += bdot(x, wu[cols, :])
+            gate_acc[...] += lax.dot_general(x, wg[:, cols], (((1,), (1,)), ((), ())), preferred_element_type=jnp.float32)
+            up_acc[...] += lax.dot_general(x, wu[:, cols], (((1,), (1,)), ((), ())), preferred_element_type=jnp.float32)
 
         @pl.when((j >= 0) & (j < Q))
         def _():
@@ -348,8 +350,7 @@
 
 def run_experts(nq, resid, ids_t, gates_t, w_gate, w_up, w_down):
     width = nq.shape[2]
-    model_width = w_gate.shape[0]
-    hidden_units = w_gate.shape[1]
+    hidden_units, model_width = w_gate.shape
     anywhere = pl.BlockSpec(memory_space=pl.ANY)
     vmem = pl.BlockSpec(memory_space=pltpu.VMEM)
     bf16, f32 = jnp.bfloat16, jnp.float32
@@ -368,8 +369,8 @@
             pltpu.VMEM((ALLROWS, hidden_units), f32),
             pltpu.VMEM((ALLROWS, hidden_units), f32),
             pltpu.VMEM((ALLROWS, hidden_units), bf16),
-            pltpu.VMEM((model_width, hidden_units), bf16),
-            pltpu.VMEM((model_width, hidden_units), bf16),
+            pltpu.VMEM((hidden_units, model_width), bf16),
+            pltpu.VMEM((hidden_units, model_width), bf16),
             pltpu.VMEM((hidden_units, model_width), bf16),
             pltpu.VMEM((Q, PEERS, ROWS, width), bf16),
             pltpu.VMEM((Q, NZ, TOK, width), f32),
@@ -387,22 +388,273 @@
     )(nq, resid, ids_t, gates_t, w_gate, w_up, w_down)
 
 
-def sent_to_all(shard, axis):
-    devices = lax.axis_size(axis)
-    return lax.all_to_all(
-        jnp.broadcast_to(shard[None], (devices, *shard.shape)), axis, 0, 0, tiled=True
-    )
-
-
-def joined_along(blocks, dim):
-    dims = list(blocks.shape[1:])
-    dims[dim] *= blocks.shape[0]
-    return jnp.moveaxis(blocks, 0, dim).reshape(dims)
-
-
-def gather_directly(shard, axis, dim):
-    blocks = sent_to_all(shard, axis)
-    return joined_along(blocks, dim)
+HEADS = 8
+NX = 4
+SEGKEYS = NY * NZ * NC
+
+
+def attend_kernel(
+    lat_hbm, q_ref, mem_ref, len_ref, hid_ref, gain_ref, wuv_hbm, wout_hbm, nq_ref, resid_ref,
+    keys, qrows, acc, top, total, wuv, wout,
+    load_sem, ksend, krecv, psend, precv, wsend, wrecv, wpsend, wprecv,
+):
+    me, y, z, c = place()
+    x = lax.axis_index("dp")
+    pos = lat_hbm.shape[1]
+    lat = lat_hbm.shape[2]
+    rows = HEADS * pos
+    partner = device_at(y, z, 1 - c)
+    own_start = pl.multiple_of(me * pos, pos)
+
+    loads = [
+        pltpu.make_async_copy(lat_hbm.at[0], keys.at[0, pl.ds(own_start, pos)], load_sem.at[0]),
+        pltpu.make_async_copy(lat_hbm.at[1], keys.at[1, pl.ds(own_start, pos)], load_sem.at[1]),
+        pltpu.make_async_copy(wout_hbm, wout.at[x], load_sem.at[2]),
+        pltpu.make_async_copy(wuv_hbm, wuv.at[x], load_sem.at[3]),
+    ]
+    for load in loads:
+        load.start()
+
+    barrier = pltpu.get_barrier_semaphore()
+    mesh_id = pl.DeviceIdType.MESH
+    expert_ids = [
+        device_at(y, wrap(z + 1, NZ), c), device_at(y, wrap(z - 1, NZ), c),
+        device_at(wrap(y + 1, NY), z, c), device_at(wrap(y - 1, NY), z, c), partner,
+    ]
+    for dev in expert_ids:
+        pl.semaphore_signal(barrier, inc=1, device_id={"expert": dev}, device_id_type=mesh_id)
+    for dev in (wrap(x + 1, NX), wrap(x - 1, NX)):
+        pl.semaphore_signal(barrier, inc=1, device_id={"dp": dev}, device_id_type=mesh_id)
+
+    def key_block(s, by, bz, bc):
+        return keys.at[s, pl.ds(pl.multiple_of(device_at(by, bz, bc) * pos, pos), pos)]
+
+    def k_copy(s, role, by, bz, to):
+        ref = key_block(s, by, bz, c)
+        block = by * NZ + bz
+        return send(ref, ref, ksend.at[s, role, block], krecv.at[s, block], to)
+
+    def p_copy(s, by, bz, bc):
+        ref = key_block(s, by, bz, bc)
+        block = by * NZ + bz
+        return send(ref, ref, psend.at[s, block], precv.at[s, block], partner)
+
+    def w_pieces(bx, bc):
+        half = wout.shape[1] // 2
+        sub = half // 2
+        first = wout.at[bx, pl.ds(pl.multiple_of(bc * half, half), sub)]
+        second = wout.at[bx, pl.ds(pl.multiple_of(bc * half + sub, sub), sub)]
+        return [first, second, wuv.at[bx, bc]]
+
+    def w_copy(bx, piece, role, to):
+        ref = w_pieces(bx, c)[piece]
+        return pltpu.make_async_remote_copy(
+            src_ref=ref, dst_ref=ref, send_sem=wsend.at[role, piece], recv_sem=wrecv.at[bx, piece],
+            device_id={"dp": to}, device_id_type=mesh_id,
+        )
+
+    def wp_copy(bx, piece, bc):
+        ref = w_pieces(bx, bc)[piece]
+        return send(ref, ref, wpsend.at[bx, piece], wprecv.at[bx, piece], partner)
+
+    rounds = [[] for _ in range(8)]
+    sends = []
+
+    def add_send(t, make):
+        sends.append(make)
+        rounds[t].append(lambda: make().start())
+
+    def add_wait(t, make):
+        rounds[t].append(lambda: make().wait_recv())
+
+    def dir_of(v):
+        return 1 - 2 * lax.rem(v, 2)
+
+    def arrived_everywhere(s, t, by, bz, second):
+        add_send(t, lambda: p_copy(s, by, bz, c))
+        if second is not None:
+            second(t, by, bz)
+
+    def along(s, t, by, bz, axis, d, first_role, then):
+        n = NZ if axis == "z" else NY
+        major, minor = n // 2, n - 1 - n // 2
+
+        def to(k):
+            return device_at(y, wrap(z + k, NZ), c) if axis == "z" else device_at(wrap(y + k, NY), z, c)
+
+        def block(k):
+            return (by, wrap(bz + k, NZ)) if axis == "z" else (wrap(by + k, NY), bz)
+
+        add_send(t, lambda: k_copy(s, first_role, by, bz, to(d)))
+        add_send(t, lambda: k_copy(s, first_role + 1, by, bz, to(-d)))
+        for h in range(1, major + 1):
+            b = block(-d * h)
+            add_wait(t + h, lambda b=b: k_copy(s, first_role, *b, me))
+            if h < major:
+                add_send(t + h, lambda b=b: k_copy(s, first_role, *b, to(d)))
+            arrived_everywhere(s, t + h, *b, then)
+            if h <= minor:
+                b2 = block(d * h)
+                add_wait(t + h, lambda b2=b2: k_copy(s, first_role, *b2, me))
+                if h < minor:
+                    add_send(t + h, lambda b2=b2: k_copy(s, first_role + 1, *b2, to(-d)))
+                arrived_everywhere(s, t + h, *b2, then)
+
+    second_a = lambda t, by, bz: along(0, t, by, bz, "y", dir_of(bz), 2, None)
+    second_b = lambda t, by, bz: along(1, t, by, bz, "z", dir_of(by), 2, None)
+    arrived_everywhere(1, 0, y, z, second_b)
+    along(1, 0, y, z, "y", 1, 0, second_b)
+    arrived_everywhere(0, 0, y, z, second_a)
+    along(0, 0, y, z, "z", 1, 0, second_a)
+
+    for piece in (2, 0, 1):
+        add_send(0, lambda piece=piece: w_copy(x, piece, 0, wrap(x + 1, NX)))
+        add_send(0, lambda piece=piece: w_copy(x, piece, 1, wrap(x - 1, NX)))
+    before, after, far = wrap(x - 1, NX), wrap(x + 1, NX), wrap(x + 2, NX)
+    for piece in (2, 0, 1):
+        for bx in (before, after):
+            add_wait(5, lambda bx=bx, piece=piece: w_copy(bx, piece, 0, x))
+            add_send(5, lambda bx=bx, piece=piece: wp_copy(bx, piece, c))
+        if piece == 1:
+            add_send(5, lambda: w_copy(after, 1, 3, before))
+        else:
+            add_send(5, lambda piece=piece: w_copy(before, piece, 2, after))
+    for piece in (2, 0, 1):
+        add_wait(7, lambda piece=piece: w_copy(far, piece, 0, x))
+        add_send(7, lambda piece=piece: wp_copy(far, piece, c))
+
+    scale = score_scale
+    for s in range(2):
+        for h in range(HEADS):
+            qrows[s, h * pos : (h + 1) * pos, :] = q_ref[s, :, h * lat : (h + 1) * lat]
+    row_pos = me * pos + lax.bitwise_and(lax.broadcasted_iota(jnp.int32, (rows, 1), 0), pos - 1)
+    contract_last = (((1,), (1,)), ((), ()))
+    for s in range(2):
+        k = mem_ref[s]
+        sc = lax.dot_general(qrows[s], k, contract_last, preferred_element_type=jnp.float32) * scale
+        m = jnp.max(sc, axis=1, keepdims=True)
+        p = jnp.exp(sc - m)
+        top[s] = jnp.broadcast_to(m, (rows, 128))
+        total[s] = jnp.broadcast_to(jnp.sum(p, axis=1, keepdims=True), (rows, 128))
+        acc[s] = bdot(p.astype(jnp.bfloat16), k)
+
+    def fold(s, bz):
+        run = NC * pos
+        k = jnp.concatenate(
+            [keys[s, pl.ds(pl.multiple_of(device_at(by, bz, 0) * pos, run), run), :] for by in range(NY)], axis=0
+        )
+        count = NY * run
+        sc = lax.dot_general(qrows[s], k, contract_last, preferred_element_type=jnp.float32) * scale
+        lane = lax.broadcasted_iota(jnp.int32, (1, count), 1)
+        key_pos = lax.shift_right_logical(lane, 7) * (NZ * run) + bz * run + lax.bitwise_and(lane, run - 1)
+        limit = jnp.minimum(row_pos + 1, len_ref[s])
+        sc = jnp.where(key_pos < limit, sc, -jnp.inf)
+        old = top[s]
+        new = jnp.maximum(old, jnp.max(sc, axis=1, keepdims=True))
+        factor = jnp.exp(old - new)
+        p = jnp.exp(sc - new[:, 0:1])
+        top[s] = new
+        total[s] = total[s] * factor + jnp.sum(p, axis=1, keepdims=True)
+        acc[s] = acc[s] * factor[:, 0:1] + bdot(p.astype(jnp.bfloat16), k)
+
+    pl.semaphore_wait(barrier, len(expert_ids) + 2)
+    for load in loads:
+        load.wait()
+
+    def round_step(t, carry):
+        for r in range(8):
+
+            @pl.when(t == r)
+            def _():
+                for act in rounds[r]:
+                    act()
+
+        u = t - 3
+
+        @pl.when(u >= 0)
+        def _():
+            count = jnp.where((u == 0) | (u == 4), 1, 2)
+
+            def piece(v, carry2):
+                bz = wrap(z + u * (1 - 2 * v), NZ)
+                for by in range(NY):
+                    for s in range(2):
+                        p_copy(s, by, bz, 1 - c).wait_recv()
+                for s in range(2):
+                    fold(s, bz)
+                return carry2
+
+            lax.fori_loop(0, count, piece, 0)
+
+        return carry
+
+    lax.fori_loop(0, 8, round_step, 0)
+
+    for bx in (before, after, far):
+        for piece in range(3):
+            wp_copy(bx, piece, 1 - c).wait_recv()
+
+    heads = []
+    per = wuv.shape[1]
+    for h in range(HEADS):
+        part = []
+        for s in range(2):
+            one = slice(h * pos, (h + 1) * pos)
+            part.append((acc[s, one, :] / total[s, one, 0:1]).astype(jnp.bfloat16))
+        mixed = jnp.concatenate(part, axis=0)
+        heads.append(bdot(mixed, wuv[h // per, h % per]).astype(jnp.bfloat16))
+    values = jnp.concatenate(heads, axis=1)
+    width = nq_ref.shape[2]
+    squares = jnp.zeros((TOK, 1), jnp.float32)
+    deep = wout.shape[0] * wout.shape[1]
+    for j in range(Q):
+        cols = slice(j * width, (j + 1) * width)
+        res = bdot(values, wout[:, :, cols].reshape(deep, width)) + hid_ref[:, cols].astype(jnp.float32)
+        resid_ref[:, cols] = res
+        squares = squares + jnp.sum(res * res, axis=1, keepdims=True)
+    rs = lax.rsqrt(squares / (Q * width) + norm_eps)
+    for j in range(Q):
+        cols = slice(j * width, (j + 1) * width)
+        nq_ref[j] = (resid_ref[:, cols] * rs * gain_ref[:, cols].astype(jnp.float32)).astype(jnp.bfloat16)
+
+    for make in sends:
+        make().wait_send()
+
+
+def run_attention(lat, q, mem, lengths, hid, gain, w_uv, w_out):
+    anywhere = pl.BlockSpec(memory_space=pl.ANY)
+    vmem = pl.BlockSpec(memory_space=pltpu.VMEM)
+    bf16, f32 = jnp.bfloat16, jnp.float32
+    dma = pltpu.SemaphoreType.DMA
+    seqs, pos, lat_dim = lat.shape
+    rows = HEADS * pos
+    model_width = hid.shape[1]
+    blocks = NY * NZ
+    return pl.pallas_call(
+        attend_kernel,
+        out_shape=(
+            jax.ShapeDtypeStruct((Q, TOK, model_width // Q), bf16),
+            jax.ShapeDtypeStruct((TOK, model_width), f32),
+        ),
+        in_specs=[anywhere, vmem, vmem, pl.BlockSpec(memory_space=pltpu.SMEM), vmem, vmem, anywhere, anywhere],
+        out_specs=(vmem, vmem),
+        scratch_shapes=[
+            pltpu.VMEM((seqs, SEGKEYS * pos, lat_dim), bf16),
+            pltpu.VMEM((seqs, rows, lat_dim), bf16),
+            pltpu.VMEM((seqs, rows, lat_dim), f32),
+            pltpu.VMEM((seqs, rows, 128), f32),
+            pltpu.VMEM((seqs, rows, 128), f32),
+            pltpu.VMEM((NX,) + w_uv.shape, bf16),
+            pltpu.VMEM((NX,) + w_out.shape, bf16),
+            dma((4,)),
+            dma((seqs, 4, blocks)), dma((seqs, blocks)), dma((seqs, blocks)), dma((seqs, blocks)),
+            dma((4, 3)), dma((NX, 3)), dma((NX, 3)), dma((NX, 3)),
+        ],
+        compiler_params=pltpu.CompilerParams(
+            collective_id=0, has_side_effects=True, vmem_limit_bytes=60 * 1024 * 1024
+        ),
+        name="attend",
+    )(lat, q, mem, lengths, hid, gain, w_uv, w_out)
 
 
 def shards(
@@ -420,89 +672,18 @@
     w_up,
     w_down,
 ):
-    local_len = hidden.shape[1]
-    seq_count = hidden.shape[2]
-    model_width = hidden.shape[3]
-    latent_dim = latents.shape[3]
-    head_count = queries.shape[3] // latent_dim
-    row_count = local_len * seq_count
-    owner_count = lax.axis_size("expert")
-    shard_index = lax.axis_index("expert")
-    own_pos = shard_index * local_len + jnp.arange(local_len, dtype=jnp.int32)
-    query_rows = queries[0].reshape(local_len, seq_count, head_count, latent_dim)
-    memory = mem_latents[0]
-    seq_limit = lengths[0]
-    mem_scores = (
-        jnp.einsum("tshl,msl->shtm", query_rows, memory, preferred_element_type=jnp.float32)
-        * score_scale
+    _, local_len, seq_count, model_width = hidden.shape
+    lat = jnp.swapaxes(latents[0], 0, 1)
+    q = jnp.swapaxes(queries[0], 0, 1)
+    mem = jnp.swapaxes(mem_latents[0], 0, 1)
+    hid = jnp.swapaxes(hidden[0], 0, 1).reshape(TOK, model_width)
+    ids_t = jnp.pad(ids[0].transpose(2, 1, 0).reshape(-1, TOK), ((0, 2), (0, 0)), constant_values=-1)
+    gates_t = jnp.pad(gates[0].transpose(2, 1, 0).reshape(-1, TOK).astype(jnp.float32), ((0, 2), (0, 0)))
+    nq, resid = run_attention(lat, q, mem, lengths[0], hid, norm_gain[None], w_uv, w_out)
+    out = run_experts(
+        nq, resid, ids_t, gates_t, jnp.swapaxes(w_gate[0], 0, 1), jnp.swapaxes(w_up[0], 0, 1), w_down[0]
     )
-    first_max = jnp.max(mem_scores, axis=3)
-    mem_weights = jnp.exp(mem_scores - first_max[..., None])
-    first_sum = jnp.sum(mem_weights, axis=3)
-    first_acc = jnp.einsum(
-        "shtm,msl->tshl",
-        mem_weights.astype(jnp.bfloat16),
-        memory,
-        preferred_element_type=jnp.float32,
-    )
-
-    def fold_step(carry, portion):
-        old_max, old_sum, old_acc = carry
-        key_rows = portion[0]
-        key_pos = jnp.arange(key_rows.shape[0], dtype=jnp.int32)
-        scores = (
-            jnp.einsum("tshl,jsl->shtj", query_rows, key_rows, preferred_element_type=jnp.float32)
-            * score_scale
-        )
-        causal = key_pos[None, :] <= own_pos[:, None]
-        inside = key_pos[None, :] < seq_limit[:, None]
-        visible = causal[None, None, :, :] & inside[:, None, None, :]
-        scores = jnp.where(visible, scores, -jnp.inf)
-        new_max = jnp.maximum(old_max, jnp.max(scores, axis=3))
-        weights = jnp.exp(scores - new_max[..., None])
-        factor = jnp.exp(old_max - new_max)
-        new_sum = old_sum * factor + jnp.sum(weights, axis=3)
-        contrib = jnp.einsum(
-            "shtj,jsl->tshl",
-            weights.astype(jnp.bfloat16),
-            key_rows,
-            preferred_element_type=jnp.float32,
-        )
-        new_acc = old_acc * jnp.transpose(factor, (2, 0, 1))[..., None] + contrib
-        return (new_max, new_sum, new_acc)
-
-    portion = lax.all_gather(latents, "expert", axis=1, tiled=True)
-    last_pos = jnp.max(own_pos)
-    final_max, final_sum, final_acc = lax.cond(
-        jnp.int32(0) <= last_pos,
-        lambda state: fold_step(state, portion),
-        lambda state: state,
-        (first_max, first_sum, first_acc),
-    )
-    attended = (final_acc / jnp.transpose(final_sum, (2, 0, 1))[..., None]).astype(jnp.bfloat16)
-    values = jnp.einsum(
-        "tshl,hlv->tshv",
-        attended,
-        gather_directly(w_uv, "dp", 0),
-        preferred_element_type=jnp.float32,
-    ).astype(jnp.bfloat16)
-    flat_values = values.reshape(row_count, -1)
-    attn_out = jnp.dot(
-        flat_values,
-        lax.all_gather(w_out, "dp", axis=0, tiled=True),
-        preferred_element_type=jnp.float32,
-    )
-    residual = hidden[0].reshape(row_count, model_width).astype(jnp.float32) + attn_out
-    mean_square = jnp.mean(residual * residual, axis=-1, keepdims=True)
-    normed = (residual * lax.rsqrt(mean_square + norm_eps) * norm_gain.astype(jnp.float32)).astype(
-        jnp.bfloat16
-    )
-    width = model_width // Q
-    nq = jnp.moveaxis(normed.reshape(row_count, Q, width), 1, 0)
-    ids_t = jnp.pad(ids[0].reshape(row_count, -1).T, ((0, 2), (0, 0)), constant_values=-1)
-    gates_t = jnp.pad(gates[0].reshape(row_count, -1).T.astype(jnp.float32), ((0, 2), (0, 0)))
-    layer_out = run_experts(nq, residual, ids_t, gates_t, w_gate[0], w_up[0], w_down[0])
-    return layer_out.reshape(1, local_len, seq_count, model_width)
+    return jnp.swapaxes(out.reshape(seq_count, local_len, model_width), 0, 1)[None]
 
 
 def solution(mesh):

time: 313 us -> 225 us (0.72)
  waiting for transfers between devices: 69.6 us -> 0 us
  Pallas kernels: 154 us -> 214 us
  matrix products: 37.7 us -> 0 us
  between operations: 14.1 us -> 0.05 us
  local copies, waits for them, and re-layouts: 23.1 us -> 9.92 us
  other arithmetic: 9.45 us -> 0.6 us
  starting transfers between devices: 4.34 us -> 0 us
    all_gather x2 -> x0, waiting for transfers between devices: 68.9 us -> none  [the longest x1 59 us: shards(): portion = lax.all_gather(latents, 'expert', axis=1, tiled=True)]
    pallas_call x0 -> x1, Pallas kernels: none -> 63.2 us  [run_attention(): pl.pallas_call(attend_kernel, out_shape=(jax.ShapeDtypeStruct((Q, TOK, mo...]
    dot_general x6 -> x0, matrix products: 37.7 us -> none  [the longest x1 15.6 us: fold_step(): jnp.einsum('tshl,jsl->shtj', query_rows, key_rows, preferred_element_type...]
    unnamed x17 -> x13, local copies, waits for them, and re-layouts: 11.2 us -> 4.18 us
    reduce_sum x2 -> x0, other arithmetic: 5.49 us -> none  [the longest x1 4.84 us: fold_step(): new_sum = old_sum * factor + jnp.sum(weights, axis=3)]
    all_to_all x1 -> x0, starting transfers between devices: 4.29 us -> none  [sent_to_all(): lax.all_to_all(jnp.broadcast_to(shard[None], (devices, *shard.shape)), ax...]
  transfers between devices with their start and end apart: 3 -> 0, of which waited for: 2 -> 0; matrix products, arithmetic and copies ran while one was open for 19% -> 0% of each run, Pallas kernels for 0% -> 0%
where the time goes in v2:
time: 225 us
  Pallas kernels  214 us (95%)
  local copies, waits for them, and re-layouts  9.92 us (4%)
    pallas_call x1, Pallas kernels, run_experts(): pl.pallas_call(expert_kernel, out_shape=jax.ShapeDtypeStruct((TOK, model_...  151 us
    pallas_call x1, Pallas kernels, run_attention(): pl.pallas_call(attend_kernel, out_shape=(jax.ShapeDtypeStruct((Q, TOK, mo...  63.2 us

profile of v2, /device:TPU:32, one launch (start us, length us, event | category | flops | bytes accessed | tf_op | source)
XLA Modules:
  0.0 225.0 jit_solution(8661788194091450036)
XLA Ops:
  0.0 0.0 copy-start
  0.0 0.0 copy-start.1
  0.0 0.0 copy-start.3
  0.0 0.0 copy-start.2
  0.0 0.0 copy-start.4
  0.0 2.9 %copy.23 = bf16[1,64,2,4096]{3,1,2,0:T(8,128)(2,1)} copy(bf16[1,64,2,4096]{3,2,1,0:T(2,128)(2,1)} %param.14) | data formatting | bytes 2097152 | tf_op args[1]
  2.9 2.0 copy.17
  4.9 0.0 copy-done
  4.9 0.7 copy.25
  5.6 0.0 copy-done.1
  5.6 0.6 copy.26
  6.2 0.0 copy-done.3
  6.2 0.6 broadcast_in_dim.6.gain_ref
  6.8 63.2 %attend.1 = (bf16[8,128,256]{2,1,0:T(8,128)(2,1)}, f32[128,2048]{1,0:T(8,128)}) custom-call(bf16[2,64,512]{2,1,0:T(8,128)(2,1)} %bitcast.45, bf16[2,64,4096]{2,1,0:T(8,128)(2,1)} %bitcast.39, bf16[2,32,512]{2,1,0:T(8,128)(2,1)} %bitcast.47, s32[2]{0:T(128)} %bitcast.50, bf16[128,2048]{1,0:T(8,128)(2,1)} %bitcast.43, ...), custom_call_target="tpu_custom_call" | custom-call | tf_op jit(solution)/shard_map/attend/pallas_call | solution.py:633
  70.0 0.0 copy-done.2
  70.0 0.1 reshape.15
  70.1 0.6 pad.10.ids_ref
  70.7 0.0 copy-done.4
  70.7 0.1 convert_element_type.14
  70.8 0.6 pad_convert_fusion.gates_ref
  71.4 151.3 %experts.1 = bf16[128,2048]{1,0:T(8,128)(2,1)} custom-call(bf16[8,128,256]{2,1,0:T(8,128)(2,1)} %get-tuple-element.7.nq_hbm, f32[128,2048]{1,0:T(8,128)} %get-tuple-element.8.resid_hbm, s32[8,128]{1,0:T(8,128)} %pad.10.ids_ref, f32[8,128]{1,0:T(8,128)} %pad_convert_fusion.gates_ref, bf16[704,2048]{1,0:T(8,128)(2,1)} %bitcast.40, bf16[704,2048]{1,0:T(8,128)(2,1)} %bitcast.41, ...), custom_call_target="tpu_custom_call" | custom-call | tf_op jit(solution)/shard_map/experts/pallas_call | solution.py:358
  222.6 2.4 %copy.24 = bf16[2,64,2048]{2,0,1:T(2,128)(2,1)} copy(bf16[2,64,2048]{2,1,0:T(8,128)(2,1)} %bitcast.44) | data formatting | bytes 1048576 | tf_op jit(solution)/shard_map/reshape | solution.py:686
Async XLA Ops:
  0.0 4.9 %copy-start = (bf16[1,64,2,512]{3,2,1,0:T(2,128)(2,1)S(1)}, bf16[1,64,2,512]{3,2,1,0:T(2,128)(2,1)}, u32[]{:S(2)}) copy-start(bf16[1,64,2,512]{3,2,1,0:T(2,128)(2,1)} %param.15) | copy-start | bytes 393220
  0.0 5.6 %copy-start.1 = (bf16[1,32,2,512]{3,2,1,0:T(2,128)(2,1)S(1)}, bf16[1,32,2,512]{3,2,1,0:T(2,128)(2,1)}, u32[]{:S(2)}) copy-start(bf16[1,32,2,512]{3,2,1,0:T(2,128)(2,1)} %param.16) | copy-start | bytes 196612
  0.0 6.2 %copy-start.3 = (bf16[2048]{0:T(1024)(128)(2,1)S(1)}, bf16[2048]{0:T(1024)(128)(2,1)}, u32[]{:S(2)}) copy-start(bf16[2048]{0:T(1024)(128)(2,1)} %param.20) | copy-start | bytes 12292
  0.0 70.0 %copy-start.2 = (s32[1,64,2,6]{1,2,3,0:T(2,128)S(1)}, s32[1,64,2,6]{1,2,3,0:T(2,128)}, u32[]{:S(2)}) copy-start(s32[1,64,2,6]{1,2,3,0:T(2,128)} %param.18) | copy-start | bytes 9220
  0.0 70.7 %copy-start.4 = (bf16[1,64,2,6]{1,2,3,0:T(2,128)(2,1)S(1)}, bf16[1,64,2,6]{1,2,3,0:T(2,128)(2,1)}, u32[]{:S(2)}) copy-start(bf16[1,64,2,6]{1,2,3,0:T(2,128)(2,1)} %param.19) | copy-start | bytes 4612

commit v3 on v2

v3 whole, which is shorter than its diff:
```python
import jax
import jax.numpy as jnp
from jax import lax
from jax.experimental import pallas as pl
from jax.experimental.pallas import tpu as pltpu
from jax.sharding import PartitionSpec as P

score_scale = 192.0 ** (-0.5)
norm_eps = 1e-06


NY, NZ, NC = 4, 8, 2
Q = 8
ADVANCE = 1
HOP1, NEAR_AT, HOP2, HOP3 = 1, 2, 2, 3
FAR_AT = HOP3 + 1
FFN_NEAR = NEAR_AT + 3
FFN_FAR = FAR_AT + 2
RET_NEAR = 2
MIX_FAR, MIX_NEAR = 2, RET_NEAR + 2
SUM1 = MIX_FAR + 1
SUM2 = MIX_NEAR
SUM3 = SUM2 + 1
LAST = SUM3 + 1
TOK = 128
CAP = 14
EXPERTS = 64
PEERS = NY * NC
ROWS = NZ * CAP
ALLROWS = PEERS * ROWS
NEAR = 4
REL = (0, -1, 1, -2, 2, -3, 3, 4)
SLOT = {r: i for i, r in enumerate(REL)}
GROUPS = NZ // NEAR
GROWS = NEAR * CAP
HALF = PEERS * GROWS


def place():
    me = lax.axis_index("expert")
    c = lax.rem(me, NC)
    z = lax.rem(lax.div(me, NC), NZ)
    y = lax.div(me, NC * NZ)
    return me, y, z, c


def device_at(y, z, c):
    return (y * NZ + z) * NC + c


def wrap(v, n):
    return lax.rem(v + 2 * n, n)


def send(src, dst, ssem, rsem, to):
    return pltpu.make_async_remote_copy(
        src_ref=src,
        dst_ref=dst,
        send_sem=ssem,
        recv_sem=rsem,
        device_id={"expert": to},
        device_id_type=pl.DeviceIdType.MESH,
    )


def bdot(a, b):
    return jnp.dot(a, b, preferred_element_type=jnp.float32)


def expert_kernel(
    nq_hbm, resid_hbm, ids_ref, gates_ref, wg_hbm, wu_hbm, wd_hbm, out_ref,
    xs, place_m, mix_m, sent, got, gate_acc, up_acc, act, wg, wu, wd, back, part, landed, resid, table,
    load_sem, zsend, zrecv, ysend, yrecv, osend, orecv, rsend, rrecv, tsend, trecv,
):
    width = xs.shape[3]
    me, y, z, c = place()
    my_slot = y * NC + c
    right = device_at(y, wrap(z + 1, NZ), c)
    left = device_at(y, wrap(z - 1, NZ), c)

    loads = [
        pltpu.make_async_copy(nq_hbm, xs.at[0], load_sem.at[0]),
        pltpu.make_async_copy(wg_hbm, wg, load_sem.at[1]),
        pltpu.make_async_copy(wu_hbm, wu, load_sem.at[2]),
        pltpu.make_async_copy(wd_hbm, wd, load_sem.at[3]),
        pltpu.make_async_copy(resid_hbm, resid, load_sem.at[4]),
    ]
    for load in loads:
        load.start()

    barrier = pltpu.get_barrier_semaphore()

    def peer(k):
        slot = wrap(my_slot + k, PEERS)
        return slot, device_at(lax.div(slot, NC), z, lax.rem(slot, NC))

    partners = [peer(k)[1] for k in range(1, PEERS)] + [right, left]
    for dev in partners:
        pl.semaphore_signal(barrier, inc=1, device_id={"expert": dev}, device_id_type=pl.DeviceIdType.MESH)

    expert_iota = lax.broadcasted_iota(jnp.int32, (EXPERTS, TOK), 0)
    hits = []
    named = jnp.zeros((EXPERTS, TOK), jnp.float32)
    for k in range(6):
        hit = expert_iota == jnp.broadcast_to(ids_ref[k : k + 1, :], (EXPERTS, TOK))
        hits.append(hit)
        named = named + jnp.where(hit, 1.0, 0.0)
    earlier = lax.broadcasted_iota(jnp.int32, (TOK, TOK), 0) < lax.broadcasted_iota(jnp.int32, (TOK, TOK), 1)
    before = bdot(named.astype(jnp.bfloat16), jnp.where(earlier, 1.0, 0.0).astype(jnp.bfloat16))
    expert_base = (expert_iota * CAP).astype(jnp.float32)
    rows = []
    for k in range(6):
        rows.append(jnp.sum(jnp.where(hits[k], before + expert_base, 0.0), axis=0, keepdims=True))
    filler = jnp.full((2, TOK), -1.0, jnp.float32)
    table[0] = jnp.concatenate(rows + [filler, gates_ref[...].astype(jnp.float32), filler], axis=0)

    gate_acc[...] = jnp.zeros_like(gate_acc)
    up_acc[...] = jnp.zeros_like(up_acc)

    pl.semaphore_wait(barrier, len(partners))
    loads[0].wait()

    def z_hop(j, h, sign):
        src = SLOT[-sign * h]
        dst = SLOT[-sign * (h + 1)] if h < 3 else SLOT[4]
        sem = 6 if h == 3 else h + (0 if sign > 0 else 3)
        return send(xs.at[src, j], xs.at[dst, j], zsend.at[j, sem], zrecv.at[j, dst], right if sign > 0 else left)

    def t_hop(h, sign):
        src = SLOT[-sign * h]
        dst = SLOT[-sign * (h + 1)] if h < 3 else SLOT[4]
        sem = 6 if h == 3 else h + (0 if sign > 0 else 3)
        return send(table.at[src], table.at[dst], tsend.at[sem], trecv.at[dst], right if sign > 0 else left)

    def z_here(j, slot):
        send(xs.at[slot, j], xs.at[slot, j], zsend.at[j, 0], zrecv.at[j, slot], right).wait_recv()

    def t_here(slot):
        send(table.at[slot], table.at[slot], tsend.at[0], trecv.at[slot], right).wait_recv()

    def y_copy(k, j, g):
        slot, to = peer(k)
        return send(sent.at[j, g, slot], got.at[j, g, my_slot], ysend.at[g, j, k], yrecv.at[g, j, my_slot], to)

    def y_here(k, j, g):
        slot, to = peer(k)
        send(sent.at[j, g, slot], got.at[j, g, slot], ysend.at[g, j, k], yrecv.at[g, j, slot], to).wait_recv()

    def o_copy(k, j, g):
        slot, to = peer(k)
        return send(sent.at[j, g, slot], back.at[j, g, my_slot], osend.at[g, j, k], orecv.at[g, j, my_slot], to)

    def o_here(k, j, g):
        slot, to = peer(k)
        send(sent.at[j, g, slot], back.at[j, g, slot], osend.at[g, j, k], orecv.at[g, j, slot], to).wait_recv()

    def parity(j):
        return lax.rem(z + j, 2)

    def build_tables(g):
        r = lax.broadcasted_iota(jnp.int32, (HALF, TOK), 0)
        group = lax.shift_right_logical(r * 9363, 17)
        within = r - group * CAP
        owner_slot = lax.shift_right_logical(group, 2)
        near = group - owner_slot * NEAR
        owner_y = lax.shift_right_logical(owner_slot, 1)
        owner_c = owner_slot - owner_y * NC
        owner = (owner_y * NZ + z) * NC + owner_c
        base = owner * CAP + within

        def one_block(b, carry):
            code = jnp.where(near == b, base, -7).astype(jnp.float32)
            rows_b = table[g * NEAR + b]
            hot = jnp.zeros((HALF, TOK), jnp.float32)
            mixed = jnp.zeros((HALF, TOK), jnp.float32)
            for k in range(6):
                hit = code == jnp.broadcast_to(rows_b[k : k + 1, :], (HALF, TOK))
                hot = jnp.where(hit, 1.0, hot)
                mixed = jnp.where(hit, jnp.broadcast_to(rows_b[8 + k : 9 + k, :], (HALF, TOK)), mixed)
            place_m[g, :, pl.ds(pl.multiple_of(b * TOK, TOK), TOK)] = hot.astype(jnp.bfloat16)
            mix_m[g, pl.ds(pl.multiple_of(b * TOK, TOK), TOK), :] = mixed.T.astype(jnp.bfloat16)
            return carry

        lax.fori_loop(0, NEAR, one_block, 0)

    def on(cond, f):
        pl.when(cond)(f)

    def valid(j):
        return (j >= 0) & (j < Q)

    def dispatch_step(i, carry):
        def own(j):
            z_hop(j, 0, 1).start()
            z_hop(j, 0, -1).start()

        @pl.when(i == 0)
        def _():
            t_hop(0, 1).start()
            t_hop(0, -1).start()
            for j in range(ADVANCE):
                own(j)

        on(i + ADVANCE < Q, lambda: own(i + ADVANCE))

        def forward(j, h, hop, here):
            here(j, SLOT[-h])
            if h < 3:
                hop(j, h, 1).start()
            here(j, SLOT[h])
            if h < 3:
                hop(j, h, -1).start()
            else:
                on(parity(j) == 1, lambda: hop(j, 3, 1).start())
                on(parity(j) == 0, lambda: hop(j, 3, -1).start())

        def compact(j, g):
            block_rows = xs[g * NEAR : (g + 1) * NEAR, j].reshape(NEAR * TOK, width)
            packed = bdot(place_m[g], block_rows).astype(jnp.bfloat16)
            sent[j, g] = packed.reshape(PEERS, GROWS, width)
            got[j, g, my_slot] = sent[j, g, my_slot]

        def ship(j, g):
            for k in range(1, PEERS):
                y_copy(k, j, g).start()

        def feed(j, g):
            for k in range(1, PEERS):
                y_here(k, j, g)
            x = got[j, g].reshape(HALF, width)
            cols = pl.ds(pl.multiple_of(j * width, width), width)
            last = (((1,), (1,)), ((), ()))
            gate_acc[g] += lax.dot_general(x, wg[:, cols], last, preferred_element_type=jnp.float32)
            up_acc[g] += lax.dot_general(x, wu[:, cols], last, preferred_element_type=jnp.float32)

        @pl.when(valid(i - HOP1))
        def _():
            forward(i - HOP1, 1, z_hop, z_here)

        for h in (1, 2, 3):
            on(i == h, lambda: forward(0, h, lambda j, k, sign: t_hop(k, sign), lambda j, slot: t_here(slot)))

        jn, j2, j3, jf = i - NEAR_AT, i - HOP2, i - HOP3, i - FAR_AT

        @pl.when(valid(jn))
        def _():
            z_here(jn, SLOT[-2])

        @pl.when(valid(j2))
        def _():
            z_hop(j2, 2, 1).start()
            z_here(j2, SLOT[2])
            z_hop(j2, 2, -1).start()

        on(valid(j3), lambda: forward(j3, 3, z_hop, z_here))
        on(i == 2, lambda: build_tables(0))

        @pl.when(i == 4)
        def _():
            t_here(SLOT[4])
            build_tables(1)

        on(valid(jn), lambda: compact(jn, 0))

        @pl.when(valid(jf))
        def _():
            z_here(jf, SLOT[4])
            compact(jf, 1)

        on(valid(jn), lambda: ship(jn, 0))

        @pl.when(i == FFN_NEAR)
        def _():
            loads[1].wait()
            loads[2].wait()

        on(valid(i - FFN_NEAR), lambda: feed(i - FFN_NEAR, 0))
        on(valid(jf), lambda: ship(jf, 1))
        on(valid(i - FFN_FAR), lambda: feed(i - FFN_FAR, 1))
        return carry

    lax.fori_loop(0, Q + FFN_FAR, dispatch_step, 0)

    g = gate_acc[...]
    act[...] = ((g / (1.0 + jnp.exp(-g))) * up_acc[...]).astype(jnp.bfloat16)
    loads[3].wait()
    loads[4].wait()

    def drain_dispatch(j, carry):
        for h in range(3):
            z_hop(j, h, 1).wait_send()
            z_hop(j, h, -1).wait_send()
        z_hop(j, 3, 1).wait_send()
        for g in range(GROUPS):
            for k in range(1, PEERS):
                y_copy(k, j, g).wait_send()
        return carry

    lax.fori_loop(0, Q, drain_dispatch, 0)
    for h in range(3):
        t_hop(h, 1).wait_send()
        t_hop(h, -1).wait_send()
    t_hop(3, 1).wait_send()

    def r_copy(j, k, to):
        return send(xs.at[k, j], landed.at[k, j], rsend.at[j, k], rrecv.at[j, k], to)

    def r_here(j, k):
        r_copy(j, k, right).wait_recv()

    def wide(j, k):
        return landed[k, j].astype(jnp.float32)

    def combine_step(i, carry):
        def make(j, g):
            cols = pl.ds(pl.multiple_of(j * width, width), width)
            made = bdot(act[g], wd[:, cols]).astype(jnp.bfloat16)
            sent[j, g] = made.reshape(PEERS, GROWS, width)
            back[j, g, my_slot] = sent[j, g, my_slot]

        def mix(j, g):
            for k in range(1, PEERS):
                o_here(k, j, g)
            mixed = bdot(mix_m[g], back[j, g].reshape(HALF, width))
            part[j, g * NEAR : (g + 1) * NEAR] = mixed.reshape(NEAR, TOK, width)

        def ship_back(j, g):
            for k in range(1, PEERS):
                o_copy(k, j, g).start()

        on(i < Q, lambda: make(i, 1))
        on(valid(i - RET_NEAR), lambda: make(i - RET_NEAR, 0))
        j0, j1, j2, j3, j4 = i - MIX_FAR, i - SUM1, i - SUM2, i - SUM3, i - LAST

        @pl.when(valid(j0))
        def _():
            mix(j0, 1)
            xs[0, j0] = part[j0, SLOT[4]].astype(jnp.bfloat16)

        @pl.when(valid(j1))
        def _():
            r_here(j1, 0)
            odd = (parity(j1) == 1).astype(jnp.float32)
            arrived = wide(j1, 0)
            xs[1, j1] = (part[j1, SLOT[3]] + arrived * odd).astype(jnp.bfloat16)
            xs[4, j1] = (part[j1, SLOT[-3]] + arrived * (1.0 - odd)).astype(jnp.bfloat16)

        on(i < Q, lambda: ship_back(i, 1))
        on(valid(i - RET_NEAR), lambda: ship_back(i - RET_NEAR, 0))

        @pl.when(valid(j0))
        def _():
            on(parity(j0) == 0, lambda: r_copy(j0, 0, right).start())
            on(parity(j0) == 1, lambda: r_copy(j0, 0, left).start())

        on(valid(i - MIX_NEAR), lambda: mix(i - MIX_NEAR, 0))

        def add_on(j, s):
            r_here(j, s - 1)
            xs[s, j] = (part[j, SLOT[4 - s]] + wide(j, s - 1)).astype(jnp.bfloat16)
            r_here(j, s + 2)
            xs[s + 3, j] = (part[j, SLOT[s - 4]] + wide(j, s + 2)).astype(jnp.bfloat16)

        def pass_on(j, s):
            r_copy(j, s, right).start()
            r_copy(j, s + 3, left).start()

        on(valid(j1), lambda: pass_on(j1, 1))
        on(valid(j3), lambda: add_on(j3, 3))
        on(valid(j2), lambda: add_on(j2, 2))
        on(valid(j3), lambda: pass_on(j3, 3))
        on(valid(j2), lambda: pass_on(j2, 2))

        @pl.when(valid(j4))
        def _():
            r_here(j4, 3)
            r_here(j4, 6)
            total = part[j4, 0] + wide(j4, 3) + wide(j4, 6)
            cols = pl.ds(pl.multiple_of(j4 * width, width), width)
            final = (resid[:, cols] + total).astype(jnp.bfloat16)
            for s in range(2):
                out_ref[:, s, cols] = final[s * (TOK // 2) : (s + 1) * (TOK // 2)]

        return carry

    lax.fori_loop(0, Q + LAST, combine_step, 0)

    def drain_combine(j, carry):
        for k in range(7):
            r_copy(j, k, right).wait_send()
        for g in range(GROUPS):
            for k in range(1, PEERS):
                o_copy(k, j, g).wait_send()
        return carry

    lax.fori_loop(0, Q, drain_combine, 0)


def run_experts(nq, resid, ids_t, gates_t, w_gate, w_up, w_down):
    width = nq.shape[2]
    hidden_units, model_width = w_gate.shape
    anywhere = pl.BlockSpec(memory_space=pl.ANY)
    vmem = pl.BlockSpec(memory_space=pltpu.VMEM)
    bf16, f32 = jnp.bfloat16, jnp.float32
    dma = pltpu.SemaphoreType.DMA
    return pl.pallas_call(
        expert_kernel,
        out_shape=jax.ShapeDtypeStruct((TOK // 2, 2, model_width), bf16),
        in_specs=[anywhere, anywhere, vmem, vmem, anywhere, anywhere, anywhere],
        out_specs=vmem,
        scratch_shapes=[
            pltpu.VMEM((NZ, Q, TOK, width), bf16),
            pltpu.VMEM((GROUPS, HALF, NEAR * TOK), bf16),
            pltpu.VMEM((GROUPS, NEAR * TOK, HALF), bf16),
            pltpu.VMEM((Q, GROUPS, PEERS, GROWS, width), bf16),
            pltpu.VMEM((Q, GROUPS, PEERS, GROWS, width), bf16),
            pltpu.VMEM((GROUPS, HALF, hidden_units), f32),
            pltpu.VMEM((GROUPS, HALF, hidden_units), f32),
            pltpu.VMEM((GROUPS, HALF, hidden_units), bf16),
            pltpu.VMEM((hidden_units, model_width), bf16),
            pltpu.VMEM((hidden_units, model_width), bf16),
            pltpu.VMEM((hidden_units, model_width), bf16),
            pltpu.VMEM((Q, GROUPS, PEERS, GROWS, width), bf16),
            pltpu.VMEM((Q, NZ, TOK, width), f32),
            pltpu.VMEM((7, Q, TOK, width), bf16),
            pltpu.VMEM((TOK, model_width), f32),
            pltpu.VMEM((NZ, 16, TOK), f32),
            dma((5,)),
            dma((Q, 7)), dma((Q, NZ)), dma((GROUPS, Q, PEERS)), dma((GROUPS, Q, PEERS)), dma((GROUPS, Q, PEERS)), dma((GROUPS, Q, PEERS)),
            dma((Q, 7)), dma((Q, 7)), dma((7,)), dma((NZ,)),
        ],
        compiler_params=pltpu.CompilerParams(
            collective_id=1, has_side_effects=True, vmem_limit_bytes=60 * 1024 * 1024
        ),
        name="experts",
    )(nq, resid, ids_t, gates_t, w_gate, w_up, w_down)


HEADS = 8
NX = 4
SEGKEYS = NY * NZ * NC


def attend_kernel(
    lat_hbm, q_ref, mem_ref, len_ref, hid_ref, gain_ref, wuv_hbm, wout_hbm, nq_ref, resid_ref,
    keys, qrows, acc, top, total, wuv, wout,
    load_sem, ksend, krecv, psend, precv, wsend, wrecv, wpsend, wprecv,
):
    me, y, z, c = place()
    x = lax.axis_index("dp")
    pos = lat_hbm.shape[0]
    lat = lat_hbm.shape[2]
    rows = HEADS * pos
    partner = device_at(y, z, 1 - c)
    own_start = pl.multiple_of(me * pos, pos)

    loads = [
        pltpu.make_async_copy(wout_hbm, wout.at[x], load_sem.at[2]),
        pltpu.make_async_copy(wuv_hbm, wuv.at[x], load_sem.at[3]),
    ]
    for load in loads:
        load.start()
    for s in range(2):
        keys[s, pl.ds(own_start, pos), :] = lat_hbm[:, s, :]

    barrier = pltpu.get_barrier_semaphore()
    mesh_id = pl.DeviceIdType.MESH
    expert_ids = [
        device_at(y, wrap(z + 1, NZ), c), device_at(y, wrap(z - 1, NZ), c),
        device_at(wrap(y + 1, NY), z, c), device_at(wrap(y - 1, NY), z, c), partner,
    ]
    for dev in expert_ids:
        pl.semaphore_signal(barrier, inc=1, device_id={"expert": dev}, device_id_type=mesh_id)
    for dev in (wrap(x + 1, NX), wrap(x - 1, NX)):
        pl.semaphore_signal(barrier, inc=1, device_id={"dp": dev}, device_id_type=mesh_id)

    def key_block(s, by, bz, bc):
        return keys.at[s, pl.ds(pl.multiple_of(device_at(by, bz, bc) * pos, pos), pos)]

    def k_copy(s, role, by, bz, to):
        ref = key_block(s, by, bz, c)
        block = by * NZ + bz
        return send(ref, ref, ksend.at[s, role, block], krecv.at[s, block], to)

    def p_copy(s, by, bz, bc):
        ref = key_block(s, by, bz, bc)
        block = by * NZ + bz
        return send(ref, ref, psend.at[s, block], precv.at[s, block], partner)

    def w_pieces(bx, bc):
        half = wout.shape[1] // 2
        sub = half // 2
        first = wout.at[bx, pl.ds(pl.multiple_of(bc * half, half), sub)]
        second = wout.at[bx, pl.ds(pl.multiple_of(bc * half + sub, sub), sub)]
        return [first, second, wuv.at[bx, bc]]

    def w_copy(bx, piece, role, to):
        ref = w_pieces(bx, c)[piece]
        return pltpu.make_async_remote_copy(
            src_ref=ref, dst_ref=ref, send_sem=wsend.at[role, piece], recv_sem=wrecv.at[bx, piece],
            device_id={"dp": to}, device_id_type=mesh_id,
        )

    def wp_copy(bx, piece, bc):
        ref = w_pieces(bx, bc)[piece]
        return send(ref, ref, wpsend.at[bx, piece], wprecv.at[bx, piece], partner)

    rounds = [[] for _ in range(8)]
    sends = []

    def add_send(t, make):
        sends.append(make)
        rounds[t].append(lambda: make().start())

    def add_wait(t, make):
        rounds[t].append(lambda: make().wait_recv())

    def dir_of(v):
        return 1 - 2 * lax.rem(v, 2)

    def arrived_everywhere(s, t, by, bz, second):
        add_send(t, lambda: p_copy(s, by, bz, c))
        if second is not None:
            second(t, by, bz)

    def along(s, t, by, bz, axis, d, first_role, then):
        n = NZ if axis == "z" else NY
        major, minor = n // 2, n - 1 - n // 2

        def to(k):
            return device_at(y, wrap(z + k, NZ), c) if axis == "z" else device_at(wrap(y + k, NY), z, c)

        def block(k):
            return (by, wrap(bz + k, NZ)) if axis == "z" else (wrap(by + k, NY), bz)

        add_send(t, lambda: k_copy(s, first_role, by, bz, to(d)))
        add_send(t, lambda: k_copy(s, first_role + 1, by, bz, to(-d)))
        for h in range(1, major + 1):
            b = block(-d * h)
            add_wait(t + h, lambda b=b: k_copy(s, first_role, *b, me))
            if h < major:
                add_send(t + h, lambda b=b: k_copy(s, first_role, *b, to(d)))
            arrived_everywhere(s, t + h, *b, then)
            if h <= minor:
                b2 = block(d * h)
                add_wait(t + h, lambda b2=b2: k_copy(s, first_role, *b2, me))
                if h < minor:
                    add_send(t + h, lambda b2=b2: k_copy(s, first_role + 1, *b2, to(-d)))
                arrived_everywhere(s, t + h, *b2, then)

    second_a = lambda t, by, bz: along(0, t, by, bz, "y", dir_of(bz), 2, None)
    second_b = lambda t, by, bz: along(1, t, by, bz, "z", dir_of(by), 2, None)
    arrived_everywhere(1, 0, y, z, second_b)
    along(1, 0, y, z, "y", 1, 0, second_b)
    arrived_everywhere(0, 0, y, z, second_a)
    along(0, 0, y, z, "z", 1, 0, second_a)

    for piece in (2, 0, 1):
        add_send(0, lambda piece=piece: w_copy(x, piece, 0, wrap(x + 1, NX)))
        add_send(0, lambda piece=piece: w_copy(x, piece, 1, wrap(x - 1, NX)))
    before, after, far = wrap(x - 1, NX), wrap(x + 1, NX), wrap(x + 2, NX)
    for piece in (2, 0, 1):
        for bx in (before, after):
            add_wait(4, lambda bx=bx, piece=piece: w_copy(bx, piece, 0, x))
            add_send(4, lambda bx=bx, piece=piece: wp_copy(bx, piece, c))
        if piece == 1:
            add_send(4, lambda: w_copy(after, 1, 3, before))
        else:
            add_send(4, lambda piece=piece: w_copy(before, piece, 2, after))
    for piece in (2, 0, 1):
        add_wait(7, lambda piece=piece: w_copy(far, piece, 0, x))
        add_send(7, lambda piece=piece: wp_copy(far, piece, c))

    scale = score_scale
    row_pos = me * pos + lax.bitwise_and(lax.broadcasted_iota(jnp.int32, (rows, 1), 0), pos - 1)
    contract_last = (((1,), (1,)), ((), ()))
    def fold(s, bz):
        run = NC * pos
        k = jnp.concatenate(
            [keys[s, pl.ds(pl.multiple_of(device_at(by, bz, 0) * pos, run), run), :] for by in range(NY)], axis=0
        )
        count = NY * run
        sc = lax.dot_general(qrows[s], k, contract_last, preferred_element_type=jnp.float32) * scale
        lane = lax.broadcasted_iota(jnp.int32, (1, count), 1)
        key_pos = lax.shift_right_logical(lane, 7) * (NZ * run) + bz * run + lax.bitwise_and(lane, run - 1)
        limit = jnp.minimum(row_pos + 1, len_ref[s])
        sc = jnp.where(key_pos < limit, sc, -jnp.inf)
        old = top[s]
        new = jnp.maximum(old, jnp.max(sc, axis=1, keepdims=True))
        factor = jnp.exp(old - new)
        p = jnp.exp(sc - new[:, 0:1])
        top[s] = new
        total[s] = total[s] * factor + jnp.sum(p, axis=1, keepdims=True)
        acc[s] = acc[s] * factor[:, 0:1] + bdot(p.astype(jnp.bfloat16), k)

    pl.semaphore_wait(barrier, len(expert_ids) + 2)
    for load in loads:
        load.wait()
    for act in rounds[0]:
        act()

    for s in range(2):
        for h in range(HEADS):
            qrows[s, h * pos : (h + 1) * pos, :] = q_ref[:, s, h * lat : (h + 1) * lat]
    for s in range(2):
        k = mem_ref[:, s, :]
        sc = lax.dot_general(qrows[s], k, contract_last, preferred_element_type=jnp.float32) * scale
        m = jnp.max(sc, axis=1, keepdims=True)
        p = jnp.exp(sc - m)
        top[s] = jnp.broadcast_to(m, (rows, 128))
        total[s] = jnp.broadcast_to(jnp.sum(p, axis=1, keepdims=True), (rows, 128))
        acc[s] = bdot(p.astype(jnp.bfloat16), k)

    def round_step(t, carry):
        for r in range(1, 7):

            @pl.when(t == r)
            def _():
                for act in rounds[r]:
                    act()

        u = t - 2

        @pl.when(u >= 0)
        def _():
            count = jnp.where((u == 0) | (u == 4), 1, 2)

            def piece(v, carry2):
                bz = wrap(z + u * (1 - 2 * v), NZ)
                for by in range(NY):
                    for s in range(2):
                        p_copy(s, by, bz, 1 - c).wait_recv()
                for s in range(2):
                    fold(s, bz)
                return carry2

            lax.fori_loop(0, count, piece, 0)

        return carry

    lax.fori_loop(1, 7, round_step, 0)
    for act in rounds[7]:
        act()

    for bx in (before, after, far):
        for piece in range(3):
            wp_copy(bx, piece, 1 - c).wait_recv()

    heads = []
    per = wuv.shape[1]
    for h in range(HEADS):
        part = []
        for s in range(2):
            one = slice(h * pos, (h + 1) * pos)
            part.append((acc[s, one, :] * (1.0 / total[s, one, 0:1])).astype(jnp.bfloat16))
        mixed = jnp.concatenate(part, axis=0)
        heads.append(bdot(mixed, wuv[h // per, h % per]).astype(jnp.bfloat16))
    values = jnp.concatenate(heads, axis=1)
    width = nq_ref.shape[2]
    squares = jnp.zeros((TOK, 1), jnp.float32)
    deep = wout.shape[0] * wout.shape[1]
    for j in range(Q):
        cols = slice(j * width, (j + 1) * width)
        res = bdot(values, wout[:, :, cols].reshape(deep, width)) + jnp.concatenate([hid_ref[:, s, cols] for s in range(2)], axis=0).astype(jnp.float32)
        resid_ref[:, cols] = res
        squares = squares + jnp.sum(res * res, axis=1, keepdims=True)
    rs = lax.rsqrt(squares / (Q * width) + norm_eps)
    for j in range(Q):
        cols = slice(j * width, (j + 1) * width)
        nq_ref[j] = (resid_ref[:, cols] * rs * gain_ref[:, cols].astype(jnp.float32)).astype(jnp.bfloat16)

    for make in sends:
        make().wait_send()


def run_attention(lat, q, mem, lengths, hid, gain, w_uv, w_out):
    anywhere = pl.BlockSpec(memory_space=pl.ANY)
    vmem = pl.BlockSpec(memory_space=pltpu.VMEM)
    bf16, f32 = jnp.bfloat16, jnp.float32
    dma = pltpu.SemaphoreType.DMA
    pos, seqs, lat_dim = lat.shape
    rows = HEADS * pos
    model_width = hid.shape[2]
    blocks = NY * NZ
    return pl.pallas_call(
        attend_kernel,
        out_shape=(
            jax.ShapeDtypeStruct((Q, TOK, model_width // Q), bf16),
            jax.ShapeDtypeStruct((TOK, model_width), f32),
        ),
        in_specs=[vmem, vmem, vmem, pl.BlockSpec(memory_space=pltpu.SMEM), vmem, vmem, anywhere, anywhere],
        out_specs=(vmem, vmem),
        scratch_shapes=[
            pltpu.VMEM((seqs, SEGKEYS * pos, lat_dim), bf16),
            pltpu.VMEM((seqs, rows, lat_dim), bf16),
            pltpu.VMEM((seqs, rows, lat_dim), f32),
            pltpu.VMEM((seqs, rows, 128), f32),
            pltpu.VMEM((seqs, rows, 128), f32),
            pltpu.VMEM((NX,) + w_uv.shape, bf16),
            pltpu.VMEM((NX,) + w_out.shape, bf16),
            dma((4,)),
            dma((seqs, 4, blocks)), dma((seqs, blocks)), dma((seqs, blocks)), dma((seqs, blocks)),
            dma((4, 3)), dma((NX, 3)), dma((NX, 3)), dma((NX, 3)),
        ],
        compiler_params=pltpu.CompilerParams(
            collective_id=0, has_side_effects=True, vmem_limit_bytes=60 * 1024 * 1024
        ),
        name="attend",
    )(lat, q, mem, lengths, hid, gain, w_uv, w_out)


def shards(
    hidden,
    queries,
    latents,
    mem_latents,
    lengths,
    ids,
    gates,
    norm_gain,
    w_uv,
    w_out,
    w_gate,
    w_up,
    w_down,
):
    _, local_len, seq_count, model_width = hidden.shape
    lat = latents[0]
    q = queries[0]
    mem = mem_latents[0]
    hid = hidden[0]
    ids_t = ids[0].transpose(2, 1, 0).reshape(-1, TOK)
    gates_t = gates[0].transpose(2, 1, 0).reshape(-1, TOK)
    nq, resid = run_attention(lat, q, mem, lengths[0], hid, norm_gain[None], w_uv, w_out)
    out = run_experts(
        nq, resid, ids_t, gates_t, jnp.swapaxes(w_gate[0], 0, 1), jnp.swapaxes(w_up[0], 0, 1), w_down[0]
    )
    return out[None]


def solution(mesh):
    return jax.shard_map(
        shards,
        mesh=mesh,
        in_specs=(
            P("dp", "expert", None, None),
            P("dp", "expert", None, None),
            P("dp", "expert", None, None),
            P("dp", None, None, None),
            P("dp", None),
            P("dp", "expert", None, None),
            P("dp", "expert", None, None),
            P(),
            P("dp", None, None),
            P("dp", None),
            P("expert", None, None),
            P("expert", None, None),
            P("expert", None, None),
        ),
        out_specs=P("dp", "expert", None, None),
        check_vma=False,
    )
```

time: 225 us -> 200 us (0.89)
  Pallas kernels: 214 us -> 192 us
  local copies, waits for them, and re-layouts: 9.92 us -> 6.2 us
    pallas_call x1, Pallas kernels: 151 us -> 131 us  [run_experts(): pl.pallas_call(expert_kernel, out_shape=jax.ShapeDtypeStruct((TOK // 2, 2...]
where the time goes in v3:
time: 200 us; the launch traced here: 198 us
  Pallas kernels  192 us (96%)
  local copies, waits for them, and re-layouts  6.2 us (3%)
    pallas_call x1, Pallas kernels, run_experts(): pl.pallas_call(expert_kernel, out_shape=jax.ShapeDtypeStruct((TOK // 2, 2...  131 us
    pallas_call x1, Pallas kernels, run_attention(): pl.pallas_call(attend_kernel, out_shape=(jax.ShapeDtypeStruct((Q, TOK, mo...  61.3 us

profile of v3, /device:TPU:32, one launch (start us, length us, event | category | flops | bytes accessed | tf_op | source)
XLA Modules:
  0.0 198.1 jit_solution(8956406311415423585)
XLA Ops:
  0.0 1.4 reshape.7.gates_ref
  1.4 1.4 reshape.6.ids_ref
  2.7 1.3 broadcast_in_dim.6.gain_ref
  4.0 61.3 %attend.1 = (bf16[8,128,256]{2,1,0:T(8,128)(2,1)}, f32[128,2048]{1,0:T(8,128)}) custom-call(bf16[64,2,512]{2,1,0:T(2,128)(2,1)} %bitcast.25, bf16[64,2,4096]{2,1,0:T(2,128)(2,1)} %bitcast.23, bf16[32,2,512]{2,1,0:T(2,128)(2,1)} %bitcast.26, s32[2]{0:T(128)} %bitcast.29, bf16[64,2,2048]{2,1,0:T(2,128)(2,1)} %bitcast.24, ...), custom_call_target="tpu_custom_call" | custom-call | tf_op jit(solution)/shard_map/attend/pallas_call | solution.py:685
  65.3 130.6 %experts.1 = bf16[64,2,2048]{2,1,0:T(2,128)(2,1)} custom-call(bf16[8,128,256]{2,1,0:T(8,128)(2,1)} %get-tuple-element.7.nq_hbm, f32[128,2048]{1,0:T(8,128)} %get-tuple-element.8.resid_hbm, s32[6,128]{1,0:T(8,128)} %reshape.6.ids_ref, bf16[6,128]{1,0:T(8,128)(2,1)} %reshape.7.gates_ref, bf16[704,2048]{1,0:T(8,128)(2,1)} %bitcast.19, ...), custom_call_target="tpu_custom_call" | custom-call | tf_op jit(solution)/shard_map/experts/pallas_call | solution.py:406
  195.9 2.2 %copy.15 = bf16[1,64,2,2048]{3,2,1,0:T(2,128)(2,1)} copy(bf16[1,64,2,2048]{3,2,1,0:T(2,128)(2,1)} %bitcast.22) | data formatting | bytes 1048576

commit v4 on v3

--- a/solution.py
+++ b/solution.py
@@ -102,7 +102,8 @@
     hits = []
     named = jnp.zeros((EXPERTS, TOK), jnp.float32)
     for k in range(6):
-        hit = expert_iota == jnp.broadcast_to(ids_ref[k : k + 1, :], (EXPERTS, TOK))
+        row = jnp.concatenate([ids_ref[k, 0:1, :], ids_ref[k, 1:2, :]], axis=1)
+        hit = expert_iota == jnp.broadcast_to(row, (EXPERTS, TOK))
         hits.append(hit)
         named = named + jnp.where(hit, 1.0, 0.0)
     earlier = lax.broadcasted_iota(jnp.int32, (TOK, TOK), 0) < lax.broadcasted_iota(jnp.int32, (TOK, TOK), 1)
@@ -112,7 +113,11 @@
     for k in range(6):
         rows.append(jnp.sum(jnp.where(hits[k], before + expert_base, 0.0), axis=0, keepdims=True))
     filler = jnp.full((2, TOK), -1.0, jnp.float32)
-    table[0] = jnp.concatenate(rows + [filler, gates_ref[...].astype(jnp.float32), filler], axis=0)
+    gate_rows = []
+    for k in range(6):
+        both = gates_ref[k].astype(jnp.float32)
+        gate_rows.append(jnp.concatenate([both[0:1], both[1:2]], axis=1))
+    table[0] = jnp.concatenate(rows + [filler] + gate_rows + [filler], axis=0)
 
     gate_acc[...] = jnp.zeros_like(gate_acc)
     up_acc[...] = jnp.zeros_like(up_acc)
@@ -274,8 +279,8 @@
             loads[1].wait()
             loads[2].wait()
 
+        on(valid(jf), lambda: ship(jf, 1))
         on(valid(i - FFN_NEAR), lambda: feed(i - FFN_NEAR, 0))
-        on(valid(jf), lambda: ship(jf, 1))
         on(valid(i - FFN_FAR), lambda: feed(i - FFN_FAR, 1))
         return carry
 
@@ -667,7 +672,7 @@
     rs = lax.rsqrt(squares / (Q * width) + norm_eps)
     for j in range(Q):
         cols = slice(j * width, (j + 1) * width)
-        nq_ref[j] = (resid_ref[:, cols] * rs * gain_ref[:, cols].astype(jnp.float32)).astype(jnp.bfloat16)
+        nq_ref[j] = (resid_ref[:, cols] * rs * gain_ref[cols].astype(jnp.float32).reshape(1, width)).astype(jnp.bfloat16)
 
     for make in sends:
         make().wait_send()
@@ -729,9 +734,9 @@
     q = queries[0]
     mem = mem_latents[0]
     hid = hidden[0]
-    ids_t = ids[0].transpose(2, 1, 0).reshape(-1, TOK)
-    gates_t = gates[0].transpose(2, 1, 0).reshape(-1, TOK)
-    nq, resid = run_attention(lat, q, mem, lengths[0], hid, norm_gain[None], w_uv, w_out)
+    ids_t = ids[0].transpose(2, 1, 0)
+    gates_t = gates[0].transpose(2, 1, 0)
+    nq, resid = run_attention(lat, q, mem, lengths[0], hid, norm_gain, w_uv, w_out)
     out = run_experts(
         nq, resid, ids_t, gates_t, jnp.swapaxes(w_gate[0], 0, 1), jnp.swapaxes(w_up[0], 0, 1), w_down[0]
     )

time: 200 us -> 196 us (0.980)
  local copies, waits for them, and re-layouts: 6.2 us -> 2.2 us
    reshape x2 -> x0, local copies, waits for them, and re-layouts: 2.72 us -> none  [the longest x1 1.36 us: shards(): gates_t = gates[0].transpose(2, 1, 0).reshape(-1, TOK)]
where the time goes in v4:
time: 196 us; the launch traced here: 194 us
  Pallas kernels  192 us (98%)
  local copies, waits for them, and re-layouts  2.2 us (1%)
    pallas_call x1, Pallas kernels, run_experts(): pl.pallas_call(expert_kernel, out_shape=jax.ShapeDtypeStruct((TOK // 2, 2...  131 us
    pallas_call x1, Pallas kernels, run_attention(): pl.pallas_call(attend_kernel, out_shape=(jax.ShapeDtypeStruct((Q, TOK, mo...  61.3 us

profile of v4, /device:TPU:32, one launch (start us, length us, event | category | flops | bytes accessed | tf_op | source)
XLA Modules:
  0.0 194.1 jit_solution(18405211577138091487)
XLA Ops:
  0.0 61.3 %attend.1 = (bf16[8,128,256]{2,1,0:T(8,128)(2,1)}, f32[128,2048]{1,0:T(8,128)}) custom-call(bf16[64,2,512]{2,1,0:T(2,128)(2,1)} %bitcast.25, bf16[64,2,4096]{2,1,0:T(2,128)(2,1)} %bitcast.23, bf16[32,2,512]{2,1,0:T(2,128)(2,1)} %bitcast.26, s32[2]{0:T(128)} %bitcast.29, bf16[64,2,2048]{2,1,0:T(2,128)(2,1)} %bitcast.24, bf16[2048]{0:T(1024)(128)(2,1)} %gain_ref.1, ...), custom_call_target="tpu_custom_call" | custom-call | tf_op jit(solution)/shard_map/attend/pallas_call | solution.py:690
  61.3 130.6 %experts.1 = bf16[64,2,2048]{2,1,0:T(2,128)(2,1)} custom-call(bf16[8,128,256]{2,1,0:T(8,128)(2,1)} %get-tuple-element.7.nq_hbm, f32[128,2048]{1,0:T(8,128)} %get-tuple-element.8.resid_hbm, s32[6,2,64]{2,1,0:T(2,128)} %bitcast.27, bf16[6,2,64]{2,1,0:T(2,128)(2,1)} %bitcast.28, bf16[704,2048]{1,0:T(8,128)(2,1)} %bitcast.19, bf16[704,2048]{1,0:T(8,128)(2,1)} %bitcast.20, ...), custom_call_target="tpu_custom_call" | custom-call | tf_op jit(solution)/shard_map/experts/pallas_call | solution.py:411
  191.9 2.2 %copy.15 = bf16[1,64,2,2048]{3,2,1,0:T(2,128)(2,1)} copy(bf16[1,64,2,2048]{3,2,1,0:T(2,128)(2,1)} %bitcast.22) | data formatting | bytes 1048576
